TPU v7x, 512 devices: a 8x2x16 block of a 8x8x16 slice. The times are simulated.
512 devices in a mesh: group: 2 (over y), ctx: 8 (over x), ep: 32 (over z, core).
Axes of the slice: x: 8, y: 2, z: 16, core: 2. Of those that a mesh axis runs over, the one named last changes fastest.
The devices are a block of a 8x8x16 slice.
Arguments:
- q_latent: bfloat16 [2048, 65536], P(('group', 'ctx'), 'ep'), parts along dimension 0, may hold values from -48 to 48
- q_rope: bfloat16 [2048, 8192], P(('group', 'ctx'), 'ep'), parts along dimension 0, may hold values from -6 to 6
- latent_keys: bfloat16 [1024, 1024], P('group', 'ctx'), parts along dimension 0, may hold values from -8 to 8
- rope_keys: bfloat16 [128, 1024], P('group', 'ctx'), parts along dimension 0, may hold values from -8 to 8
- w_uv: bfloat16 [128, 512, 128], P('ep'), may hold values from -0.25 to 0.25
- moe_tokens: bfloat16 [16384, 7168], P(('group', 'ep'), 'ctx'), parts along dimension 0, may hold values from -6 to 6
- norm_gain: float32 [7168], P('ctx'), may hold values from 0.1 to 1.9
- expert_ids: int32 [16384, 2], P(('group', 'ep')), parts along dimension 0, may hold values from 0 to 15, all different within a row; in each aligned block of 256 rows (0 to 255, 256 to 511, ...) at most 48 rows name the same one
- route_scale: float32 [16384, 2], P(('group', 'ep')), parts along dimension 0, may hold values from 0.5 to 2.5
- w_gate: bfloat16 [32, 7168, 512], P('ep', 'ctx'), may hold values from -0.0625 to 0.0625
- w_up: bfloat16 [32, 7168, 512], P('ep', 'ctx'), may hold values from -0.0625 to 0.0625
- w_down: bfloat16 [32, 512, 7168], P('ep', None, 'ctx'), may hold values from -0.1875 to 0.1875
Outputs:
- attn_out: bfloat16 [2048, 16384], P(('group', 'ctx'), 'ep'), parts along dimension 0
- moe_out: bfloat16 [16384, 7168], P(('group', 'ep'), 'ctx'), parts along dimension 0
There are 2 independent parts, one for each index of `group`. A program takes and returns all parts, laid end to end along the dimension named above; an argument that names none is the same for every part. Nothing has to cross between parts.
Inputs may be any that keep to these rules, and one draw needn't show every extreme that they name: `expert_ids`: each row names 2 different experts; among the rows of one ep index no expert is named more than 48 times, a bound that some block reaches.
All inputs are finite; a program needn't handle non-finite values.
Results may differ from a plain program's by a relative error of at most 0.024.
Values may be sent and summed in bfloat16 or wider, within the bound.
No kernel may reach another device: no remote copies, remote signals or barrier semaphores. Data moves between devices by JAX's collectives and lax.ppermute only.
A program may use at most 64 MiB of HBM per device.

v0:
```python
import jax
import jax.numpy as jnp
from jax import lax
from jax.sharding import PartitionSpec as P

score_scale = 192.0 ** (-0.5)
norm_eps = 1e-06
neg_large = -1e30


def in_one_piece(arrays, axis, dim, along):
    ends, at = ([], 0)
    for a in arrays[:-1]:
        at += a.shape[along]
        ends.append(at)
    both = jnp.concatenate(arrays, axis=along)
    return tuple(jnp.split(lax.all_gather(both, axis, axis=dim, tiled=True), ends, axis=along))


def sent_to_all(value, axis):
    count = lax.axis_size(axis)
    return lax.all_to_all(
        jnp.broadcast_to(value[None], (count, *value.shape)), axis, 0, 0, tiled=True
    )


def of_everyone(value, axis):
    everything = sent_to_all(value, axis)
    return jnp.sum(everything, axis=0)


def in_order(blocks, dim):
    blocks = jnp.moveaxis(blocks, 0, dim)
    dims = blocks.shape
    return blocks.reshape(*dims[:dim], dims[dim] * dims[dim + 1], *dims[dim + 2 :])


def collect(value, axis, dim):
    return in_order(sent_to_all(value, axis), dim)


def body(
    q_latent,
    q_rope,
    latent_keys,
    rope_keys,
    w_uv,
    moe_tokens,
    norm_gain,
    expert_ids,
    route_scale,
    w_gate,
    w_up,
    w_down,
):
    seq_rows = q_latent.shape[0]
    head_count = w_uv.shape[0]
    latent_dim = latent_keys.shape[0]
    rope_dim = rope_keys.shape[0]
    query_lat = (
        q_latent.reshape(seq_rows, head_count, latent_dim)
        .transpose(1, 0, 2)
        .reshape(head_count * seq_rows, latent_dim)
    )
    query_rot = (
        q_rope.reshape(seq_rows, head_count, rope_dim)
        .transpose(1, 0, 2)
        .reshape(head_count * seq_rows, rope_dim)
    )
    query_pos = lax.axis_index("ctx") * seq_rows + jnp.tile(
        jnp.arange(seq_rows, dtype=jnp.int32), head_count
    )
    total_rows = head_count * seq_rows
    run_max = jnp.full((total_rows, 1), neg_large, jnp.float32)
    lat_piece, rope_piece = in_one_piece((latent_keys, rope_keys), "ctx", 1, 0)
    piece_width = lat_piece.shape[1]
    scores = jnp.dot(query_lat, lat_piece, preferred_element_type=jnp.float32)
    scores = (
        scores + jnp.dot(query_rot, rope_piece, preferred_element_type=jnp.float32)
    ) * score_scale
    key_pos = jnp.arange(piece_width, dtype=jnp.int32)
    visible = key_pos[None, :] <= query_pos[:, None]
    masked = jnp.where(visible, scores, neg_large)
    new_max = jnp.maximum(run_max, jnp.max(masked, axis=1, keepdims=True))
    weights = jnp.where(visible, jnp.exp(masked - new_max), 0.0)
    new_sum = jnp.sum(weights, axis=1, keepdims=True)
    update = lax.dot_general(
        weights.astype(jnp.bfloat16),
        lat_piece,
        (((1,), (1,)), ((), ())),
        preferred_element_type=jnp.float32,
    )
    context = (update / new_sum).astype(jnp.bfloat16).reshape(head_count, seq_rows, latent_dim)
    attn_heads = jnp.einsum("hsl,hlv->shv", context, w_uv, preferred_element_type=jnp.float32)
    attn_out = attn_heads.reshape(seq_rows, head_count * w_uv.shape[2]).astype(jnp.bfloat16)
    tokens_wide = moe_tokens.astype(jnp.float32)
    local_sq = jnp.sum(tokens_wide * tokens_wide, axis=1)
    total_sq = of_everyone(local_sq, "ctx")
    model_width = moe_tokens.shape[1] * lax.axis_size("ctx")
    scale_rows = lax.rsqrt(total_sq / model_width + norm_eps)
    normed = (tokens_wide * scale_rows[:, None] * norm_gain[None, :]).astype(jnp.bfloat16)
    tok_rows, top_count = expert_ids.shape
    expert_count = lax.axis_size("ep") // 2
    capacity = min(tok_rows, 3 * tok_rows * top_count // (2 * expert_count))
    flat_ids = expert_ids.reshape(-1)
    onehot = (flat_ids[:, None] == jnp.arange(expert_count, dtype=jnp.int32)[None, :]).astype(
        jnp.int32
    )
    slot_index = jnp.sum((jnp.cumsum(onehot, axis=0) - onehot) * onehot, axis=1)
    target_slot = flat_ids * capacity + slot_index
    place_map = (
        target_slot[:, None] == jnp.arange(expert_count * capacity, dtype=jnp.int32)[None, :]
    ).astype(jnp.float32)
    place_map = place_map.reshape(tok_rows, top_count, expert_count * capacity)
    route_map = jnp.sum(place_map, axis=1)
    weight_map = jnp.sum(place_map * route_scale[:, :, None], axis=1)
    send_rows = jnp.dot(
        route_map.T.astype(jnp.bfloat16), normed, preferred_element_type=jnp.float32
    ).astype(jnp.bfloat16)
    send_rows = jnp.repeat(send_rows.reshape(expert_count, capacity, -1), 2, axis=0)
    arrived = lax.all_to_all(send_rows, "ep", split_axis=0, concat_axis=0, tiled=True)
    rows_in = arrived.reshape(-1, arrived.shape[2])
    gate_w = w_gate[0]
    up_w = w_up[0]
    down_w = w_down[0]
    gate_part = jnp.dot(rows_in, gate_w, preferred_element_type=jnp.float32)
    up_part = jnp.dot(rows_in, up_w, preferred_element_type=jnp.float32)
    row_share = lax.psum_scatter(
        jnp.concatenate([gate_part, up_part], axis=1).astype(jnp.bfloat16),
        "ctx",
        scatter_dimension=0,
        tiled=True,
    ).astype(jnp.float32)
    half_width = gate_w.shape[1]
    part_hidden = (jax.nn.silu(row_share[:, :half_width]) * row_share[:, half_width:]).astype(
        jnp.bfloat16
    )
    hidden = collect(part_hidden, "ctx", 0)
    expert_out = (
        jnp.dot(hidden, down_w, preferred_element_type=jnp.float32)
        .astype(jnp.bfloat16)
        .reshape(arrived.shape)
    )
    returned = lax.all_to_all(expert_out, "ep", split_axis=0, concat_axis=0, tiled=True)
    pair_flat = (
        returned.astype(jnp.float32)
        .reshape(expert_count, 2, capacity, -1)
        .sum(axis=1)
        .reshape(expert_count * capacity, -1)
    )
    moe_out = jnp.dot(weight_map, pair_flat, preferred_element_type=jnp.float32).astype(
        jnp.bfloat16
    )
    return (attn_out, moe_out)


def solution(mesh):
    return jax.shard_map(
        body,
        mesh=mesh,
        in_specs=(
            P(("group", "ctx"), "ep"),
            P(("group", "ctx"), "ep"),
            P("group", "ctx"),
            P("group", "ctx"),
            P("ep", None, None),
            P(("group", "ep"), "ctx"),
            P("ctx"),
            P(("group", "ep"), None),
            P(("group", "ep"), None),
            P("ep", "ctx", None),
            P("ep", "ctx", None),
            P("ep", None, "ctx"),
        ),
        out_specs=(P(("group", "ctx"), "ep"), P(("group", "ep"), "ctx")),
        check_vma=False,
    )
```

profile of v0, /device:TPU:65, one launch (start us, length us, event | category | flops | bytes accessed | tf_op | source)
XLA Modules:
  0.0 449.0 jit_solution(2984712006408799343)
XLA Ops:
  7.2 1.3 fusion.9
  9.1 7.9 %all-to-all-start = ((f32[8,1,256]{2,1,0:T(1,128)}), f32[8,1,256]{2,1,0:T(1,128)S(1)}, u32[]{:S(2)}, u32[]{:S(2)}) async-start(f32[8,1,256]{2,1,0:T(1,128)} %broadcast_in_dim.18), calls=%async_computation | async-start | bytes 16384 | tf_op jit(solution)/shard_map/all_to_all | solution.py:22
  17.0 0.8 copy.88
  18.2 1.2 reduce-window.6
  20.6 1.1 convert_reduce_fusion.1
  21.7 1.9 all-to-all-done
  24.5 174.5 %all_to_all.21 = bf16[32,48,896]{2,1,0:T(8,128)(2,1)S(1)} all-to-all(bf16[32,48,896]{2,1,0:T(8,128)(2,1)S(1)} %bitcast.66), channel_id=1, replica_groups=mesh['group'=2,'ctx'=8,'ep'=32] {'ep'}, dimensions={0} | all-to-all | bytes 5505024 | tf_op jit(solution)/shard_map/all_to_all | solution.py:121
  199.0 1.9 convolution_convert_fusion.1
  200.9 1.9 convolution_convert_fusion.2
  202.8 1.9 pad_maximum_fusion
  204.7 4.6 %copy.96 = bf16[1536,1024]{1,0:T(8,128)(2,1)} copy(bf16[1536,1024]{0,1:T(8,128)(2,1)} %pad_maximum_fusion) | data formatting | bytes 6291456
  209.4 39.7 %reduce-scatter.4.cloned.1.call-done = bf16[192,1024]{1,0:T(8,128)(2,1)} async-done(((bf16[1536,1024]{1,0:T(8,128)(2,1)}), bf16[192,1024]{1,0:T(8,128)(2,1)}) %reduce-scatter.4.cloned.1.call-update) | async-done | bytes 393232
  249.1 1.2 copy.97
  250.8 40.3 %all_to_all.22 = bf16[8,192,512]{2,1,0:T(8,128)(2,1)S(1)} all-to-all(bf16[8,192,512]{2,1,0:T(8,128)(2,1)S(1)} %broadcast_in_dim.20), channel_id=1, replica_groups=mesh['group'=2,'ctx'=8,'ep'=32] {'ctx'}, dimensions={0} | all-to-all | bytes 3145728 | tf_op jit(solution)/shard_map/all_to_all | solution.py:22
  291.2 3.4 convolution_convert_fusion
  294.5 18.7 %all-to-all-start.3 = ((bf16[32,48,896]{2,1,0:T(8,128)(2,1)}), bf16[32,48,896]{2,1,0:T(8,128)(2,1)}, u32[]{:S(2)}, u32[]{:S(2)}) async-start(bf16[32,48,896]{2,1,0:T(8,128)(2,1)} %bitcast.69), calls=%async_computation.3 | async-start | bytes 5505024 | tf_op jit(solution)/shard_map/all_to_all | solution.py:144
  314.9 40.2 %all-gather.2.cloned.1.call-done = bf16[576,1024]{1,0:T(8,128)(2,1)} async-done(((bf16[576,128]{1,0:T(8,128)(2,1)}), bf16[576,1024]{1,0:T(8,128)(2,1)}) %all-gather.2.cloned.1.call-update) | async-done | bytes 1179664 | tf_op jit(solution)/shard_map/all_gather | solution.py:17
  355.1 1.5 fusion.20
  356.5 0.9 fusion.29
  358.0 0.8 fusion.2
  359.4 0.8 copy.94
  360.2 78.4 %all-to-all-done.3 = bf16[32,48,896]{2,1,0:T(8,128)(2,1)} async-done(((bf16[32,48,896]{2,1,0:T(8,128)(2,1)}), bf16[32,48,896]{2,1,0:T(8,128)(2,1)}, u32[]{:S(2)}, u32[]{:S(2)}) %all-to-all-start.3) | async-done | bytes 2752544 | tf_op jit(solution)/shard_map/all_to_all | solution.py:144
  438.6 2.2 convert_reduce_fusion
  440.8 1.3 fusion.30
  (53 shorter events, 6.5 us)
Async XLA Ops:
  7.2 284.0 %copy-start = (bf16[1,512,896]{2,1,0:T(8,128)(2,1)S(1)}, bf16[1,512,896]{2,1,0:T(8,128)(2,1)}, u32[]{:S(2)}) copy-start(bf16[1,512,896]{2,1,0:T(8,128)(2,1)} %param.23) | copy-start | bytes 2752516
  7.2 16.4 %copy-start.1 = (bf16[256,896]{1,0:T(8,128)(2,1)S(1)}, bf16[256,896]{1,0:T(8,128)(2,1)}, u32[]{:S(2)}) copy-start(bf16[256,896]{1,0:T(8,128)(2,1)} %param.17) | copy-start | bytes 1376260
  7.2 16.4 %copy-start.8 = (f32[896]{0:T(1024)S(1)}, f32[896]{0:T(1024)}, u32[]{:S(2)}) copy-start(f32[896]{0:T(1024)} %param.18) | copy-start | bytes 10756
  9.1 14.4 %all-to-all-start = ((f32[8,1,256]{2,1,0:T(1,128)}), f32[8,1,256]{2,1,0:T(1,128)S(1)}, u32[]{:S(2)}, u32[]{:S(2)}) async-start(f32[8,1,256]{2,1,0:T(1,128)} %broadcast_in_dim.18), calls=%async_computation | async-start | bytes 16384 | tf_op jit(solution)/shard_map/all_to_all | solution.py:22
  17.0 232.2 %reduce-scatter.4.cloned.1.call-start = ((), (), s32[]{:S(2)}) async-start(), calls=%async_computation.6 | async-start | bytes 3538944
  24.5 174.5 %copy-start.9 = (bf16[1,896,512]{2,1,0:T(8,128)(2,1)S(1)}, bf16[1,896,512]{2,1,0:T(8,128)(2,1)}, u32[]{:S(2)}) copy-start(bf16[1,896,512]{2,1,0:T(8,128)(2,1)} %param.22) | copy-start | bytes 2752516
  199.0 1.9 copy-start.10
  294.5 19.0 %copy-start.4 = (bf16[512,128]{1,0:T(8,128)(2,1)S(1)}, bf16[512,128]{1,0:T(8,128)(2,1)}, u32[]{:S(2)}) copy-start(bf16[512,128]{1,0:T(8,128)(2,1)} %param.14) | copy-start | bytes 393220
  294.5 19.0 %copy-start.6 = (bf16[64,128]{1,0:T(8,128)(2,1)S(1)}, bf16[64,128]{1,0:T(8,128)(2,1)}, u32[]{:S(2)}) copy-start(bf16[64,128]{1,0:T(8,128)(2,1)} %param.15) | copy-start | bytes 49156
  294.5 19.7 %copy-start.5 = (bf16[128,256]{1,0:T(8,128)(2,1)S(1)}, bf16[128,256]{1,0:T(8,128)(2,1)}, u32[]{:S(2)}) copy-start(bf16[128,256]{1,0:T(8,128)(2,1)} %param.13) | copy-start | bytes 196612
  294.5 19.9 %copy-start.2 = (bf16[128,2048]{1,0:T(8,128)(2,1)S(1)}, bf16[128,2048]{1,0:T(8,128)(2,1)}, u32[]{:S(2)}) copy-start(bf16[128,2048]{1,0:T(8,128)(2,1)} %param.12) | copy-start | bytes 1572868
  294.5 144.1 %all-to-all-start.3 = ((bf16[32,48,896]{2,1,0:T(8,128)(2,1)}), bf16[32,48,896]{2,1,0:T(8,128)(2,1)}, u32[]{:S(2)}, u32[]{:S(2)}) async-start(bf16[32,48,896]{2,1,0:T(8,128)(2,1)} %bitcast.69), calls=%async_computation.3 | async-start | bytes 5505024 | tf_op jit(solution)/shard_map/all_to_all | solution.py:144
  313.2 41.8 %all-gather.2.cloned.1.call-start = ((), (), s32[]{:S(2)}) async-start(), calls=%async_computation.5 | async-start | bytes 1327104 | tf_op jit(solution)/shard_map/all_gather | solution.py:17
  355.1 1.5 copy-start.7
  358.0 1.0 copy-start.3
Sparse Core Ops, SparseCore 0:
  209.5 39.5 reduce-scatter.3
  316.7 38.3 all-gather.1
where the time goes:
time: 450 us; the launch traced here: 449 us
  blocking collectives  215 us (48%)
  waiting for transfers between devices  160 us (36%)
  starting transfers between devices  26.9 us (6%)
  between operations  14.3 us (3%)
  matrix products  12.7 us (3%)
  local copies, waits for them, and re-layouts  10.1 us (2%)
  other arithmetic  9.9 us (2%)
    all_to_all x1, blocking collectives, body(): lax.all_to_all(send_rows, 'ep', split_axis=0, concat_axis=0, tiled=True)  174 us
    all_to_all x1, waiting for transfers between devices, body(): lax.all_to_all(expert_out, 'ep', split_axis=0, concat_axis=0, tiled=True)  78.4 us
    all_to_all x1, blocking collectives, sent_to_all(): lax.all_to_all(jnp.broadcast_to(value[None], (count, *value.shape)), axis...  40.3 us
    all_gather x1, waiting for transfers between devices, in_one_piece(): lax.all_gather(both, axis, axis=dim, tiled=True)  40.2 us
    unnamed x3, waiting for transfers between devices  39.8 us
    all_to_all x1, starting transfers between devices, body(): lax.all_to_all(expert_out, 'ep', split_axis=0, concat_axis=0, tiled=True)  18.7 us
  transfers between devices with their start and end apart: 4, of which 4 were waited for; matrix products, arithmetic and copies ran while one was open for 2% of the time, Pallas kernels for 0%

commit v1 on v0

v1 whole, which is shorter than its diff:
```python
import jax
import jax.numpy as jnp
from jax import lax
from jax.sharding import PartitionSpec as P

score_scale = 192.0 ** (-0.5)
norm_eps = 1e-06
neg_large = -1e30
lanes = 128


def in_one_piece(arrays, axis, dim, along):
    ends, at = ([], 0)
    for a in arrays[:-1]:
        at += a.shape[along]
        ends.append(at)
    both = jnp.concatenate(arrays, axis=along)
    return tuple(jnp.split(lax.all_gather(both, axis, axis=dim, tiled=True), ends, axis=along))


def same_core(axis):
    count = lax.axis_size(axis)
    return [list(range(core, count, 2)) for core in range(2)]


def of_other_core(value, axis):
    count = lax.axis_size(axis)
    return lax.ppermute(value, axis, [(i, i ^ 1) for i in range(count)])


def attention(q_latent, q_rope, lat_piece, rope_piece, w_uv):
    seq_rows = q_latent.shape[0]
    head_count, latent_dim = w_uv.shape[:2]
    rope_dim = rope_piece.shape[0]
    query_lat = (
        q_latent.reshape(seq_rows, head_count, latent_dim)
        .transpose(1, 0, 2)
        .reshape(head_count * seq_rows, latent_dim)
    )
    query_rot = (
        q_rope.reshape(seq_rows, head_count, rope_dim)
        .transpose(1, 0, 2)
        .reshape(head_count * seq_rows, rope_dim)
    )
    query_pos = lax.axis_index("ctx") * seq_rows + jnp.tile(
        jnp.arange(seq_rows, dtype=jnp.int32), head_count
    )
    scores = jnp.dot(query_lat, lat_piece, preferred_element_type=jnp.float32)
    scores = (
        scores + jnp.dot(query_rot, rope_piece, preferred_element_type=jnp.float32)
    ) * score_scale
    key_pos = jnp.arange(lat_piece.shape[1], dtype=jnp.int32)
    visible = key_pos[None, :] <= query_pos[:, None]
    masked = jnp.where(visible, scores, neg_large)
    row_max = jnp.max(masked, axis=1, keepdims=True)
    weights = jnp.where(visible, jnp.exp(masked - row_max), 0.0)
    row_sum = jnp.sum(weights, axis=1, keepdims=True)
    update = lax.dot_general(
        weights.astype(jnp.bfloat16),
        lat_piece,
        (((1,), (1,)), ((), ())),
        preferred_element_type=jnp.float32,
    )
    context = (update / row_sum).astype(jnp.bfloat16).reshape(head_count, seq_rows, latent_dim)
    attn_heads = jnp.einsum("hsl,hlv->shv", context, w_uv, preferred_element_type=jnp.float32)
    return attn_heads.reshape(seq_rows, head_count * w_uv.shape[2]).astype(jnp.bfloat16)


def body(
    q_latent,
    q_rope,
    latent_keys,
    rope_keys,
    w_uv,
    moe_tokens,
    norm_gain,
    expert_ids,
    route_scale,
    w_gate,
    w_up,
    w_down,
):
    lat_piece, rope_piece = in_one_piece((latent_keys, rope_keys), "ctx", 1, 0)
    model_width = moe_tokens.shape[1] * lax.axis_size("ctx")
    half_width = w_gate.shape[2]
    own_in = jnp.concatenate([w_gate[0], w_up[0]], axis=1)
    in_w = jnp.concatenate([own_in, of_other_core(own_in, "ep")], axis=1)
    down_w = jnp.concatenate([w_down[0], of_other_core(w_down[0], "ep")], axis=0)

    tok_rows, top_count = expert_ids.shape
    expert_count = lax.axis_size("ep") // 2
    capacity = min(tok_rows, 3 * tok_rows * top_count // (2 * expert_count))
    flat_ids = expert_ids.reshape(-1)
    onehot = (flat_ids[:, None] == jnp.arange(expert_count, dtype=jnp.int32)[None, :]).astype(
        jnp.int32
    )
    slot_index = jnp.sum((jnp.cumsum(onehot, axis=0) - onehot) * onehot, axis=1)
    target_slot = flat_ids * capacity + slot_index
    place_map = (
        target_slot[:, None] == jnp.arange(expert_count * capacity, dtype=jnp.int32)[None, :]
    ).astype(jnp.float32)
    place_map = place_map.reshape(tok_rows, top_count, expert_count * capacity)
    route_map = jnp.sum(place_map, axis=1)
    weight_map = jnp.sum(place_map * route_scale[:, :, None], axis=1)
    send_rows = jnp.dot(
        route_map.T.astype(jnp.bfloat16), moe_tokens, preferred_element_type=jnp.float32
    ).astype(jnp.bfloat16)
    arrived = lax.all_to_all(
        send_rows.reshape(expert_count, capacity, -1),
        "ep",
        split_axis=0,
        concat_axis=0,
        tiled=True,
        axis_index_groups=same_core("ep"),
    )
    rows_in = arrived.reshape(-1, arrived.shape[2])
    rows_wide = rows_in.astype(jnp.float32)
    row_sq = jnp.sum(rows_wide * rows_wide, axis=1, keepdims=True)
    gained = (rows_wide * norm_gain[None, :]).astype(jnp.bfloat16)
    in_part = jnp.dot(gained, in_w, preferred_element_type=jnp.float32).astype(jnp.bfloat16)
    row_share = lax.psum_scatter(
        jnp.concatenate(
            [in_part, jnp.broadcast_to(row_sq, (row_sq.shape[0], lanes)).astype(jnp.bfloat16)], axis=1
        ),
        "ctx",
        scatter_dimension=0,
        tiled=True,
    ).astype(jnp.float32)
    row_scale = lax.rsqrt(row_share[:, -1:] / model_width + norm_eps)
    sums = row_share[:, :-lanes] * row_scale
    part_hidden = jnp.concatenate(
        [
            jax.nn.silu(sums[:, at : at + half_width]) * sums[:, at + half_width : at + 2 * half_width]
            for at in (0, 2 * half_width)
        ],
        axis=1,
    ).astype(jnp.bfloat16)
    hidden = lax.all_gather(part_hidden, "ctx", axis=0, tiled=True)
    expert_out = (
        jnp.dot(hidden, down_w, preferred_element_type=jnp.float32)
        .astype(jnp.bfloat16)
        .reshape(arrived.shape)
    )
    returned = lax.all_to_all(
        expert_out,
        "ep",
        split_axis=0,
        concat_axis=0,
        tiled=True,
        axis_index_groups=same_core("ep"),
    ).reshape(expert_count * capacity, -1)
    weight_high = weight_map.astype(jnp.bfloat16)
    weight_low = (weight_map - weight_high.astype(jnp.float32)).astype(jnp.bfloat16)
    moe_out = (
        jnp.dot(weight_high, returned, preferred_element_type=jnp.float32)
        + jnp.dot(weight_low, returned, preferred_element_type=jnp.float32)
    ).astype(jnp.bfloat16)
    attn_out = attention(q_latent, q_rope, lat_piece, rope_piece, w_uv)
    return (attn_out, moe_out)


def solution(mesh):
    return jax.shard_map(
        body,
        mesh=mesh,
        in_specs=(
            P(("group", "ctx"), "ep"),
            P(("group", "ctx"), "ep"),
            P("group", "ctx"),
            P("group", "ctx"),
            P("ep", None, None),
            P(("group", "ep"), "ctx"),
            P("ctx"),
            P(("group", "ep"), None),
            P(("group", "ep"), None),
            P("ep", "ctx", None),
            P("ep", "ctx", None),
            P("ep", None, "ctx"),
        ),
        out_specs=(P(("group", "ctx"), "ep"), P(("group", "ep"), "ctx")),
        check_vma=False,
    )
```

time: 450 us -> 315 us (0.70)
  the two profiles are of different devices: /device:TPU:65 before, /device:TPU:66 now
where the time goes in v1:
time: 315 us
  waiting for transfers between devices  205 us (65%)
  starting transfers between devices  61.2 us (19%)
  matrix products  16.3 us (5%)
  between operations  14.1 us (4%)
  other arithmetic  12 us (4%)
  local copies, waits for them, and re-layouts  6.3 us (2%)
    all_to_all x1, waiting for transfers between devices, body(): lax.all_to_all(send_rows.reshape(expert_count, capacity, -1), 'ep', split...  61 us
    reduce_scatter x1, waiting for transfers between devices, body(): lax.psum_scatter(jnp.concatenate([in_part, jnp.broadcast_to(row_sq, (row_...  49.5 us
    all_gather x1, waiting for transfers between devices, in_one_piece(): lax.all_gather(both, axis, axis=dim, tiled=True)  44.7 us
    all_to_all x1, starting transfers between devices, body(): lax.all_to_all(send_rows.reshape(expert_count, capacity, -1), 'ep', split...  43.7 us
    all_gather x1, waiting for transfers between devices, body(): hidden = lax.all_gather(part_hidden, 'ctx', axis=0, tiled=True)  42.3 us
    all_to_all x1, starting transfers between devices, body(): lax.all_to_all(expert_out, 'ep', split_axis=0, concat_axis=0, tiled=True,...  13.2 us
  transfers between devices with their start and end apart: 7, of which 6 were waited for; matrix products, arithmetic and copies ran while one was open for 4% of the time, Pallas kernels for 0%

profile of v1, /device:TPU:66, one launch (start us, length us, event | category | flops | bytes accessed | tf_op | source)
XLA Modules:
  0.0 314.6 jit_solution(16068774822585044478)
XLA Ops:
  7.2 0.9 copy.57
  8.4 1.2 reduce-window.6
  10.8 1.1 select_reduce_fusion
  12.0 1.7 convolution_convert_fusion
  13.7 43.7 %all-to-all-start = ((bf16[16,48,896]{2,1,0:T(8,128)(2,1)}), bf16[16,48,896]{2,1,0:T(8,128)(2,1)S(1)}, u32[]{:S(2)}, u32[]{:S(2)}) async-start(bf16[16,48,896]{2,1,0:T(8,128)(2,1)} %bitcast.59), calls=%async_computation | async-start | bytes 2752512 | tf_op jit(solution)/shard_map/all_to_all | solution.py:108
  57.5 2.9 pad_maximum_fusion.1
  60.4 1.9 collective-permute-start
  62.3 61.0 %all-to-all-done = bf16[16,48,896]{2,1,0:T(8,128)(2,1)S(1)} async-done(((bf16[16,48,896]{2,1,0:T(8,128)(2,1)}), bf16[16,48,896]{2,1,0:T(8,128)(2,1)S(1)}, u32[]{:S(2)}, u32[]{:S(2)}) %all-to-all-start) | async-done | bytes 1376288 | tf_op jit(solution)/shard_map/all_to_all | solution.py:108
  125.2 4.9 %fusion.6 = bf16[768,2048]{1,0:T(8,128)(2,1)S(1)} fusion(bf16[768,896]{1,0:T(8,128)(2,1)S(1)} %fusion.9, bf16[896,1024]{1,0:T(8,128)(2,1)} %collective-permute-done, bf16[896,512]{1,0:T(8,128)(2,1)S(1)} %bitcast.63, bf16[896,512]{1,0:T(8,128)(2,1)S(1)} %bitcast.65), kind=kOutput, calls=%fused_computation.6 | convolution fusion | flops 2831155200 | bytes 8192000 | tf_op jit(solution)/shard_map/dot_general | solution.py:120
  130.3 2.0 pad_maximum_fusion
  132.5 49.5 %reduce-scatter.2.cloned.1.call-done = bf16[96,2176]{1,0:T(8,128)(2,1)} async-done(((bf16[768,2176]{1,0:T(8,128)(2,1)}), bf16[96,2176]{1,0:T(8,128)(2,1)}) %reduce-scatter.2.cloned.1.call-update) | async-done | bytes 417808 | tf_op jit(solution)/shard_map/reduce_scatter | solution.py:121
  182.0 1.1 convert_element_type.92
  184.2 2.0 collective-permute-start.1
  186.2 2.4 collective-permute-done.1
  188.6 42.3 %all-gather.5.cloned.1.call-done = bf16[768,1024]{1,0:T(8,128)(2,1)} async-done(((bf16[96,1024]{1,0:T(8,128)(2,1)}), bf16[768,1024]{1,0:T(8,128)(2,1)}) %all-gather.5.cloned.1.call-update) | async-done | bytes 1572880 | tf_op jit(solution)/shard_map/all_gather | solution.py:138
  230.9 4.3 %fusion.14 = bf16[768,896]{1,0:T(8,128)(2,1)} fusion(bf16[768,1024]{1,0:T(8,128)(2,1)} %all-gather.5.cloned.1.call-done, bf16[512,896]{1,0:T(8,128)(2,1)S(1)} %collective-permute-done.1, bf16[512,896]{1,0:T(8,128)(2,1)S(1)} %bitcast.71), kind=kOutput, calls=%fused_computation.19 | convolution fusion | flops 1413644288 | bytes 4784128 | tf_op jit(solution)/shard_map/dot_general | solution.py:140
  235.2 13.2 %all-to-all-start.1 = ((bf16[16,48,896]{2,1,0:T(8,128)(2,1)}), bf16[16,48,896]{2,1,0:T(8,128)(2,1)S(1)}, u32[]{:S(2)}, u32[]{:S(2)}) async-start(bf16[16,48,896]{2,1,0:T(8,128)(2,1)} %bitcast.61), calls=%async_computation.2 | async-start | bytes 2752512 | tf_op jit(solution)/shard_map/all_to_all | solution.py:144
  249.6 1.3 copy.52
  250.9 1.0 copy.53
  251.9 44.7 %all-gather.3.cloned.1.call-done = bf16[576,1024]{1,0:T(8,128)(2,1)} async-done(((bf16[576,128]{1,0:T(8,128)(2,1)}), bf16[576,1024]{1,0:T(8,128)(2,1)}) %all-gather.3.cloned.1.call-update) | async-done | bytes 1179664 | tf_op jit(solution)/shard_map/all_gather | solution.py:18
  296.6 1.5 fusion.33
  298.1 0.9 fusion.47
  301.5 4.7 %all-to-all-done.1 = bf16[16,48,896]{2,1,0:T(8,128)(2,1)S(1)} async-done(((bf16[16,48,896]{2,1,0:T(8,128)(2,1)}), bf16[16,48,896]{2,1,0:T(8,128)(2,1)S(1)}, u32[]{:S(2)}, u32[]{:S(2)}) %all-to-all-start.1) | async-done | bytes 1376288 | tf_op jit(solution)/shard_map/all_to_all | solution.py:144
  306.8 1.3 fusion.20
  (55 shorter events, 9.0 us)
Async XLA Ops:
  7.2 293.2 %copy-start = (bf16[4,512,128]{2,1,0:T(8,128)(2,1)S(1)}, bf16[4,512,128]{2,1,0:T(8,128)(2,1)}, u32[]{:S(2)}) copy-start(bf16[4,512,128]{2,1,0:T(8,128)(2,1)} %param.16) | copy-start | bytes 1572868
  7.2 4.8 %copy-start.4 = (bf16[256,896]{1,0:T(8,128)(2,1)S(1)}, bf16[256,896]{1,0:T(8,128)(2,1)}, u32[]{:S(2)}) copy-start(bf16[256,896]{1,0:T(8,128)(2,1)} %param.17) | copy-start | bytes 1376260
  13.7 109.7 %all-to-all-start = ((bf16[16,48,896]{2,1,0:T(8,128)(2,1)}), bf16[16,48,896]{2,1,0:T(8,128)(2,1)S(1)}, u32[]{:S(2)}, u32[]{:S(2)}) async-start(bf16[16,48,896]{2,1,0:T(8,128)(2,1)} %bitcast.59), calls=%async_computation | async-start | bytes 2752512 | tf_op jit(solution)/shard_map/all_to_all | solution.py:108
  57.4 124.6 %reduce-scatter.2.cloned.1.call-start = ((), (), s32[]{:S(2)}) async-start(), calls=%async_computation.4 | async-start | bytes 3760128 | tf_op jit(solution)/shard_map/reduce_scatter | solution.py:121
  57.4 66.3 %copy-start.9 = (f32[896]{0:T(1024)S(1)}, f32[896]{0:T(1024)}, u32[]{:S(2)}) copy-start(f32[896]{0:T(1024)} %param.18) | copy-start | bytes 10756
  60.4 63.7 %collective-permute-start = (bf16[896,1024]{1,0:T(8,128)(2,1)}, bf16[896,1024]{1,0:T(8,128)(2,1)}, u32[]{:S(2)}, u32[]{:S(2)}) collective-permute-start(bf16[896,1024]{1,0:T(8,128)(2,1)} %pad_maximum_fusion.1), channel_id=1, source_target_pairs={{0,1},{1,0},{2,3},{3,2},{4,5},{5,4},{6,7},{7,6},{8,9},{9,8},{10,11... | collective-permute-start | bytes 5505032 | tf_op jit(solution)/shard_map/ppermute | solution.py:28
  123.8 1.2 copy-start.1
  123.8 1.4 copy-start.2
  132.4 51.8 %copy-start.10 = (bf16[1,512,896]{2,1,0:T(8,128)(2,1)S(1)}, bf16[1,512,896]{2,1,0:T(8,128)(2,1)}, u32[]{:S(2)}) copy-start(bf16[1,512,896]{2,1,0:T(8,128)(2,1)} %param.23) | copy-start | bytes 2752516
  132.4 98.5 %all-gather.5.cloned.1.call-start = ((), (), s32[]{:S(2)}) async-start(), calls=%async_computation.5 | async-start | bytes 1769472 | tf_op jit(solution)/shard_map/all_gather | solution.py:138
  184.2 4.4 %collective-permute-start.1 = (bf16[512,896]{1,0:T(8,128)(2,1)S(1)}, bf16[512,896]{1,0:T(8,128)(2,1)S(1)}, u32[]{:S(2)}, u32[]{:S(2)}) collective-permute-start(bf16[512,896]{1,0:T(8,128)(2,1)S(1)} %bitcast.70), channel_id=1, source_target_pairs={{0,1},{1,0},{2,3},{3,2},{4,5},{5,4},{6,7},{7,6},{8,9},{9,8},{10,11... | collective-permute-start | bytes 2752520 | tf_op jit(solution)/shard_map/ppermute | solution.py:28
  235.2 13.5 %copy-start.5 = (bf16[512,128]{1,0:T(8,128)(2,1)S(1)}, bf16[512,128]{1,0:T(8,128)(2,1)}, u32[]{:S(2)}) copy-start(bf16[512,128]{1,0:T(8,128)(2,1)} %param.14) | copy-start | bytes 393220
  235.2 13.5 %copy-start.7 = (bf16[64,128]{1,0:T(8,128)(2,1)S(1)}, bf16[64,128]{1,0:T(8,128)(2,1)}, u32[]{:S(2)}) copy-start(bf16[64,128]{1,0:T(8,128)(2,1)} %param.15) | copy-start | bytes 49156
  235.2 14.2 %copy-start.6 = (bf16[128,256]{1,0:T(8,128)(2,1)S(1)}, bf16[128,256]{1,0:T(8,128)(2,1)}, u32[]{:S(2)}) copy-start(bf16[128,256]{1,0:T(8,128)(2,1)} %param.13) | copy-start | bytes 196612
  235.2 71.0 %all-to-all-start.1 = ((bf16[16,48,896]{2,1,0:T(8,128)(2,1)}), bf16[16,48,896]{2,1,0:T(8,128)(2,1)S(1)}, u32[]{:S(2)}, u32[]{:S(2)}) async-start(bf16[16,48,896]{2,1,0:T(8,128)(2,1)} %bitcast.61), calls=%async_computation.2 | async-start | bytes 2752512 | tf_op jit(solution)/shard_map/all_to_all | solution.py:144
  248.4 48.2 %all-gather.3.cloned.1.call-start = ((), (), s32[]{:S(2)}) async-start(), calls=%async_computation.3 | async-start | bytes 1327104 | tf_op jit(solution)/shard_map/all_gather | solution.py:18
  251.9 46.2 %copy-start.3 = (bf16[4,128,512]{2,1,0:T(8,128)(2,1)S(1)}, bf16[4,128,512]{2,1,0:T(8,128)(2,1)}, u32[]{:S(2)}) copy-start(bf16[4,128,512]{2,1,0:T(8,128)(2,1)} %copy.53) | copy-start | bytes 1572868
  296.6 1.5 copy-start.8
Sparse Core Ops, SparseCore 0:
  132.5 49.4 reduce-scatter.1
  184.6 46.2 all-gather.4
  251.9 44.7 all-gather.2

commit v2 on v1

--- a/solution.py
+++ b/solution.py
@@ -64,6 +64,45 @@
     context = (update / row_sum).astype(jnp.bfloat16).reshape(head_count, seq_rows, latent_dim)
     attn_heads = jnp.einsum("hsl,hlv->shv", context, w_uv, preferred_element_type=jnp.float32)
     return attn_heads.reshape(seq_rows, head_count * w_uv.shape[2]).astype(jnp.bfloat16)
+
+
+def sent_rows(route_map, tokens):
+    return jnp.dot(route_map.T, tokens, preferred_element_type=jnp.float32).astype(jnp.bfloat16)
+
+
+def to_same_core(rows, count):
+    return lax.all_to_all(
+        rows.reshape(count, -1, rows.shape[1]),
+        "ep",
+        split_axis=0,
+        concat_axis=0,
+        tiled=True,
+        axis_index_groups=same_core("ep"),
+    ).reshape(rows.shape)
+
+
+def activation_sums(rows, norm_gain, in_w):
+    rows_wide = rows.astype(jnp.float32)
+    row_sq = jnp.sum(rows_wide * rows_wide, axis=1, keepdims=True)
+    gained = (rows_wide * norm_gain[None, :]).astype(jnp.bfloat16)
+    in_part = jnp.dot(gained, in_w, preferred_element_type=jnp.float32)
+    column = lax.broadcasted_iota(jnp.int32, in_part.shape, 1)
+    in_part = jnp.where(column < in_w.shape[1] - lanes, in_part, row_sq).astype(jnp.bfloat16)
+    return lax.psum_scatter(in_part, "ctx", scatter_dimension=0, tiled=True)
+
+
+def activations(row_share, model_width, half_width):
+    row_share = row_share.astype(jnp.float32)
+    row_scale = lax.rsqrt(row_share[:, -1:] / model_width + norm_eps)
+    sums = row_share[:, :-lanes] * row_scale
+    part_hidden = jnp.concatenate(
+        [
+            jax.nn.silu(sums[:, at : at + half_width]) * sums[:, at + half_width : at + 2 * half_width]
+            for at in (0, 2 * half_width)
+        ],
+        axis=1,
+    ).astype(jnp.bfloat16)
+    return lax.all_gather(part_hidden, "ctx", axis=0, tiled=True)
 
 
 def body(
@@ -83,80 +122,70 @@
     lat_piece, rope_piece = in_one_piece((latent_keys, rope_keys), "ctx", 1, 0)
     model_width = moe_tokens.shape[1] * lax.axis_size("ctx")
     half_width = w_gate.shape[2]
-    own_in = jnp.concatenate([w_gate[0], w_up[0]], axis=1)
-    in_w = jnp.concatenate([own_in, of_other_core(own_in, "ep")], axis=1)
-    down_w = jnp.concatenate([w_down[0], of_other_core(w_down[0], "ep")], axis=0)
 
     tok_rows, top_count = expert_ids.shape
     expert_count = lax.axis_size("ep") // 2
     capacity = min(tok_rows, 3 * tok_rows * top_count // (2 * expert_count))
+    chunk = capacity // 2
+    chunk_rows = expert_count * chunk
     flat_ids = expert_ids.reshape(-1)
     onehot = (flat_ids[:, None] == jnp.arange(expert_count, dtype=jnp.int32)[None, :]).astype(
         jnp.int32
     )
     slot_index = jnp.sum((jnp.cumsum(onehot, axis=0) - onehot) * onehot, axis=1)
-    target_slot = flat_ids * capacity + slot_index
+    target_slot = (slot_index // chunk) * chunk_rows + flat_ids * chunk + slot_index % chunk
     place_map = (
-        target_slot[:, None] == jnp.arange(expert_count * capacity, dtype=jnp.int32)[None, :]
+        target_slot[:, None] == jnp.arange(2 * chunk_rows, dtype=jnp.int32)[None, :]
     ).astype(jnp.float32)
-    place_map = place_map.reshape(tok_rows, top_count, expert_count * capacity)
-    route_map = jnp.sum(place_map, axis=1)
+    place_map = place_map.reshape(tok_rows, top_count, 2 * chunk_rows)
+    route_map = jnp.sum(place_map, axis=1).astype(jnp.bfloat16)
     weight_map = jnp.sum(place_map * route_scale[:, :, None], axis=1)
-    send_rows = jnp.dot(
-        route_map.T.astype(jnp.bfloat16), moe_tokens, preferred_element_type=jnp.float32
-    ).astype(jnp.bfloat16)
-    arrived = lax.all_to_all(
-        send_rows.reshape(expert_count, capacity, -1),
-        "ep",
-        split_axis=0,
-        concat_axis=0,
-        tiled=True,
-        axis_index_groups=same_core("ep"),
-    )
-    rows_in = arrived.reshape(-1, arrived.shape[2])
-    rows_wide = rows_in.astype(jnp.float32)
-    row_sq = jnp.sum(rows_wide * rows_wide, axis=1, keepdims=True)
-    gained = (rows_wide * norm_gain[None, :]).astype(jnp.bfloat16)
-    in_part = jnp.dot(gained, in_w, preferred_element_type=jnp.float32).astype(jnp.bfloat16)
-    row_share = lax.psum_scatter(
-        jnp.concatenate(
-            [in_part, jnp.broadcast_to(row_sq, (row_sq.shape[0], lanes)).astype(jnp.bfloat16)], axis=1
-        ),
-        "ctx",
-        scatter_dimension=0,
-        tiled=True,
-    ).astype(jnp.float32)
-    row_scale = lax.rsqrt(row_share[:, -1:] / model_width + norm_eps)
-    sums = row_share[:, :-lanes] * row_scale
-    part_hidden = jnp.concatenate(
+    weight_high = weight_map.astype(jnp.bfloat16)
+    weight_low = (weight_map - weight_high.astype(jnp.float32)).astype(jnp.bfloat16)
+
+    with jax.named_scope("go_a"):
+        rows_a = to_same_core(sent_rows(route_map[:, :chunk_rows], moe_tokens), expert_count)
+    send_b = sent_rows(route_map[:, chunk_rows:], moe_tokens)
+    in_w = jnp.concatenate(
         [
-            jax.nn.silu(sums[:, at : at + half_width]) * sums[:, at + half_width : at + 2 * half_width]
-            for at in (0, 2 * half_width)
+            w_gate[0],
+            w_up[0],
+            of_other_core(w_gate[0], "ep"),
+            of_other_core(w_up[0], "ep"),
+            jnp.zeros((w_gate.shape[1], lanes), jnp.bfloat16),
         ],
         axis=1,
-    ).astype(jnp.bfloat16)
-    hidden = lax.all_gather(part_hidden, "ctx", axis=0, tiled=True)
-    expert_out = (
-        jnp.dot(hidden, down_w, preferred_element_type=jnp.float32)
-        .astype(jnp.bfloat16)
-        .reshape(arrived.shape)
-    )
-    returned = lax.all_to_all(
-        expert_out,
-        "ep",
-        split_axis=0,
-        concat_axis=0,
-        tiled=True,
-        axis_index_groups=same_core("ep"),
-    ).reshape(expert_count * capacity, -1)
-    weight_high = weight_map.astype(jnp.bfloat16)
-    weight_low = (weight_map - weight_high.astype(jnp.float32)).astype(jnp.bfloat16)
-    moe_out = (
-        jnp.dot(weight_high, returned, preferred_element_type=jnp.float32)
-        + jnp.dot(weight_low, returned, preferred_element_type=jnp.float32)
-    ).astype(jnp.bfloat16)
+    )
+    down_w = jnp.concatenate([w_down[0], of_other_core(w_down[0], "ep")], axis=0)
+    rows_a, send_b, in_w, down_w, lat_piece, rope_piece = lax.optimization_barrier(
+        (rows_a, send_b, in_w, down_w, lat_piece, rope_piece)
+    )
+    with jax.named_scope("go_b"):
+        rows_b = to_same_core(send_b, expert_count)
+    with jax.named_scope("sum_a"):
+        share_a = activation_sums(rows_a, norm_gain, in_w)
     attn_out = attention(q_latent, q_rope, lat_piece, rope_piece, w_uv)
-    return (attn_out, moe_out)
+    with jax.named_scope("sum_b"):
+        share_b = activation_sums(rows_b, norm_gain, in_w)
+    with jax.named_scope("act_a"):
+        hidden_a = activations(share_a, model_width, half_width)
+    with jax.named_scope("down_a"):
+        out_a = jnp.dot(hidden_a, down_w, preferred_element_type=jnp.float32).astype(jnp.bfloat16)
+    with jax.named_scope("back_a"):
+        back_a = to_same_core(out_a, expert_count)
+    with jax.named_scope("act_b"):
+        hidden_b = activations(share_b, model_width, half_width)
+    with jax.named_scope("down_b"):
+        out_b = jnp.dot(hidden_b, down_w, preferred_element_type=jnp.float32).astype(jnp.bfloat16)
+    with jax.named_scope("back_b"):
+        back_b = to_same_core(out_b, expert_count)
+    moe_out = jnp.zeros((tok_rows, moe_tokens.shape[1]), jnp.float32)
+    for at, back in ((0, back_a), (chunk_rows, back_b)):
+        for part in (weight_high, weight_low):
+            moe_out = moe_out + jnp.dot(
+                part[:, at : at + chunk_rows], back, preferred_element_type=jnp.float32
+            )
+    return (attn_out, moe_out.astype(jnp.bfloat16))
 
 
 def solution(mesh):

time: 315 us -> 306 us (0.971)
  waiting for transfers between devices: 205 us -> 96 us
  blocking collectives: 0 us -> 53.1 us
  starting transfers between devices: 61.2 us -> 89.3 us
  local copies, waits for them, and re-layouts: 6.3 us -> 15.3 us
  matrix products: 16.3 us -> 24.6 us
    all_gather x0 -> x2, blocking collectives: none -> 53.1 us  [activations(): return lax.all_gather(part_hidden, 'ctx', axis=0, tiled=True)]
    all_gather x1 -> x0, waiting for transfers between devices: 42.3 us -> none  [body(): hidden = lax.all_gather(part_hidden, 'ctx', axis=0, tiled=True)]
    reduce_scatter x1 -> x2, waiting for transfers between devices: 49.5 us -> 21.1 us  [activation_sums(): return lax.psum_scatter(in_part, 'ctx', scatter_dimension=0, tiled=True)]
    all_to_all x2 -> x4, waiting for transfers between devices: 65.7 us -> 39 us  [to_same_core(): lax.all_to_all(rows.reshape(count, -1, rows.shape[1]), 'ep', split_axis=0...]
    all_to_all x2 -> x4, starting transfers between devices: 56.9 us -> 82.6 us  [to_same_core(): lax.all_to_all(rows.reshape(count, -1, rows.shape[1]), 'ep', split_axis=0...]
    all_gather x1, waiting for transfers between devices: 44.7 us -> 35.7 us  [in_one_piece(): lax.all_gather(both, axis, axis=dim, tiled=True)]
    dot_general x5 -> x10, matrix products: 12.8 us -> 21.1 us  [the longest x2 10.7 us: activation_sums(): in_part = jnp.dot(gained, in_w, preferred_element_type=jnp.float32)]
    unnamed x26 -> x30, local copies, waits for them, and re-layouts: 4.31 us -> 9.14 us
  transfers between devices with their start and end apart: 7 -> 10, of which waited for: 6 -> 5; matrix products, arithmetic and copies ran while one was open for 4% -> 14% of each run, Pallas kernels for 0% -> 0%
where the time goes in v2:
time: 306 us; the launch traced here: 305 us
  waiting for transfers between devices  96 us (31%)
  starting transfers between devices  89.3 us (29%)
  blocking collectives  53.1 us (17%)
  matrix products  24.6 us (8%)
  local copies, waits for them, and re-layouts  15.3 us (5%)
  between operations  14.1 us (5%)
  other arithmetic  12.4 us (4%)
    all_to_all x4, starting transfers between devices, to_same_core(): lax.all_to_all(rows.reshape(count, -1, rows.shape[1]), 'ep', split_axis=0...  82.6 us
    all_gather x2, blocking collectives, activations(): return lax.all_gather(part_hidden, 'ctx', axis=0, tiled=True)  53.1 us
    all_to_all x4, waiting for transfers between devices, to_same_core(): lax.all_to_all(rows.reshape(count, -1, rows.shape[1]), 'ep', split_axis=0...  39 us
    all_gather x1, waiting for transfers between devices, in_one_piece(): lax.all_gather(both, axis, axis=dim, tiled=True)  35.7 us
    reduce_scatter x2, waiting for transfers between devices, activation_sums(): return lax.psum_scatter(in_part, 'ctx', scatter_dimension=0, tiled=True)  21.1 us
    dot_general x2, matrix products, activation_sums(): in_part = jnp.dot(gained, in_w, preferred_element_type=jnp.float32)  10.7 us
    unnamed x30, local copies, waits for them, and re-layouts  9.14 us
    ppermute x3, starting transfers between devices, of_other_core(): return lax.ppermute(value, axis, [(i, i ^ 1) for i in range(count)])  6.47 us
  transfers between devices with their start and end apart: 10, of which 5 were waited for; matrix products, arithmetic and copies ran while one was open for 14% of the time, Pallas kernels for 0%

profile of v2, /device:TPU:66, one launch (start us, length us, event | category | flops | bytes accessed | tf_op | source)
XLA Modules:
  0.0 304.9 jit_solution(4879207017985592927)
XLA Ops:
  11.4 2.1 select_reduce_fusion
  14.8 43.7 %all-to-all-start = ((bf16[16,24,896]{2,1,0:T(8,128)(2,1)}), bf16[16,24,896]{2,1,0:T(8,128)(2,1)S(1)}, u32[]{:S(2)}, u32[]{:S(2)}) async-start(bf16[16,24,896]{2,1,0:T(8,128)(2,1)} %bitcast.2), calls=%async_computation | async-start | bytes 1376256 | tf_op jit(solution)/shard_map/go_a/all_to_all | solution.py:74
  59.3 2.1 collective-permute-start
  61.4 2.4 collective-permute-start.1
  63.8 2.0 collective-permute-start.2
  65.8 2.3 constant_dynamic-update-slice_fusion.3
  73.3 1.4 pad_maximum_fusion
  74.7 35.7 %all-gather.2.cloned.1.call-done = bf16[576,1024]{1,0:T(8,128)(2,1)} async-done(((bf16[576,128]{1,0:T(8,128)(2,1)}), bf16[576,1024]{1,0:T(8,128)(2,1)}) %all-gather.2.cloned.1.call-update) | async-done | bytes 1179664 | tf_op jit(solution)/shard_map/all_gather | solution.py:18
  111.7 1.6 split.9
  113.5 13.1 %all-to-all-start.2 = ((bf16[16,24,896]{2,1,0:T(8,128)(2,1)}), bf16[16,24,896]{2,1,0:T(8,128)(2,1)S(1)}, u32[]{:S(2)}, u32[]{:S(2)}) async-start(bf16[16,24,896]{2,1,0:T(8,128)(2,1)} %bitcast.79), calls=%async_computation.3 | async-start | bytes 1376256 | tf_op jit(solution)/shard_map/go_b/all_to_all | solution.py:74
  126.7 5.3 %fusion = bf16[384,2176]{1,0:T(8,128)(2,1)} fusion(bf16[896,2176]{1,0:T(8,128)(2,1)} %broadcast_dynamic-update-slice_fusion, bf16[384]{0:T(512)(128)(2,1)S(1)} %fusion.5, pred[2176]{0:T(1024)(128)(4,1)S(1)} %iota_compare_fusion.4, bf16[384,896]{1,0:T(8,128)(2,1)S(1)} %bitcast.78, f32[896]{0:T(1024)S(1)} %copy-done.10), kind=kOutput, calls=%fused_computation.2 | convolution fusion | flops 1499234304 | bytes 6265216 | tf_op jit(solution)/shard_map/sum_a/dot_general | solution.py:88
  132.1 25.2 %all-to-all-done.2 = bf16[16,24,896]{2,1,0:T(8,128)(2,1)S(1)} async-done(((bf16[16,24,896]{2,1,0:T(8,128)(2,1)}), bf16[16,24,896]{2,1,0:T(8,128)(2,1)S(1)}, u32[]{:S(2)}, u32[]{:S(2)}) %all-to-all-start.2) | async-done | bytes 688160 | tf_op jit(solution)/shard_map/go_b/all_to_all | solution.py:74
  157.7 5.4 %fusion.1 = bf16[384,2176]{1,0:T(8,128)(2,1)} fusion(bf16[384,896]{1,0:T(8,128)(2,1)S(1)} %fusion.6, bf16[896,2176]{1,0:T(8,128)(2,1)} %broadcast_dynamic-update-slice_fusion, bf16[384]{0:T(512)(128)(2,1)S(1)} %broadcast_in_dim.41, pred[2176]{0:T(1024)(128)(4,1)S(1)} %iota_compare_fusion.4), kind=kOutput, calls=%fused_computation.3 | convolution fusion | flops 1498202112 | bytes 6261632 | tf_op jit(solution)/shard_map/sum_b/dot_general | solution.py:88
  163.2 14.3 %reduce-scatter.3.cloned.1.call-done = bf16[48,2176]{1,0:T(8,128)(2,1)} async-done(((bf16[384,2176]{1,0:T(8,128)(2,1)}), bf16[48,2176]{1,0:T(8,128)(2,1)}) %reduce-scatter.3.cloned.1.call-update) | async-done | bytes 208912 | tf_op jit(solution)/shard_map/sum_a/reduce_scatter | solution.py:91
  178.8 26.7 %all_gather.10 = bf16[384,1024]{1,0:T(8,128)(2,1)S(1)} all-gather(bf16[48,1024]{1,0:T(8,128)(2,1)S(1)} %pad_maximum_fusion.2), channel_id=1, replica_groups=mesh['group'=2,'ctx'=8,'ep'=32] {'ctx'}, dimensions={0}, use_global_device_ids=true | all-gather | bytes 884736 | tf_op jit(solution)/shard_map/act_a/all_gather | solution.py:105
  205.6 1.8 convolution_convert_fusion.1
  207.4 13.2 %all-to-all-start.1 = ((bf16[16,24,896]{2,1,0:T(8,128)(2,1)}), bf16[16,24,896]{2,1,0:T(8,128)(2,1)S(1)}, u32[]{:S(2)}, u32[]{:S(2)}) async-start(bf16[16,24,896]{2,1,0:T(8,128)(2,1)} %bitcast.87), calls=%async_computation.2 | async-start | bytes 1376256 | tf_op jit(solution)/shard_map/back_a/all_to_all | solution.py:74
  220.5 6.8 %reduce-scatter.5.cloned.1.call-done = bf16[48,2176]{1,0:T(8,128)(2,1)} async-done(((bf16[384,2176]{1,0:T(8,128)(2,1)}), bf16[48,2176]{1,0:T(8,128)(2,1)}) %reduce-scatter.5.cloned.1.call-update) | async-done | bytes 208912 | tf_op jit(solution)/shard_map/sum_b/reduce_scatter | solution.py:91
  228.8 26.4 %all_gather.11 = bf16[384,1024]{1,0:T(8,128)(2,1)S(1)} all-gather(bf16[48,1024]{1,0:T(8,128)(2,1)S(1)} %pad_maximum_fusion.3), channel_id=1, replica_groups=mesh['group'=2,'ctx'=8,'ep'=32] {'ctx'}, dimensions={0}, use_global_device_ids=true | all-gather | bytes 884736 | tf_op jit(solution)/shard_map/act_b/all_gather | solution.py:105
  255.2 1.8 convolution_convert_fusion
  257.1 12.7 %all-to-all-start.3 = ((bf16[16,24,896]{2,1,0:T(8,128)(2,1)}), bf16[16,24,896]{2,1,0:T(8,128)(2,1)S(1)}, u32[]{:S(2)}, u32[]{:S(2)}) async-start(bf16[16,24,896]{2,1,0:T(8,128)(2,1)} %bitcast.86), calls=%async_computation.5 | async-start | bytes 1376256 | tf_op jit(solution)/shard_map/back_b/all_to_all | solution.py:74
  273.0 2.4 subtract_convert_fusion
  275.4 1.4 fusion.26
  282.0 13.8 %all-to-all-done.3 = bf16[16,24,896]{2,1,0:T(8,128)(2,1)S(1)} async-done(((bf16[16,24,896]{2,1,0:T(8,128)(2,1)}), bf16[16,24,896]{2,1,0:T(8,128)(2,1)S(1)}, u32[]{:S(2)}, u32[]{:S(2)}) %all-to-all-start.3) | async-done | bytes 688160 | tf_op jit(solution)/shard_map/back_b/all_to_all | solution.py:74
  (87 shorter events, 27.2 us)
Async XLA Ops:
  7.2 271.9 %copy-start = (bf16[4,512,128]{2,1,0:T(8,128)(2,1)S(1)}, bf16[4,512,128]{2,1,0:T(8,128)(2,1)}, u32[]{:S(2)}) copy-start(bf16[4,512,128]{2,1,0:T(8,128)(2,1)} %param.16) | copy-start | bytes 1572868
  7.2 6.3 %copy-start.3 = (bf16[256,896]{1,0:T(8,128)(2,1)S(1)}, bf16[256,896]{1,0:T(8,128)(2,1)}, u32[]{:S(2)}) copy-start(bf16[256,896]{1,0:T(8,128)(2,1)} %param.17) | copy-start | bytes 1376260
  10.4 48.1 %copy-start.8 = (bf16[512,128]{1,0:T(8,128)(2,1)S(1)}, bf16[512,128]{1,0:T(8,128)(2,1)}, u32[]{:S(2)}) copy-start(bf16[512,128]{1,0:T(8,128)(2,1)} %param.14) | copy-start | bytes 393220
  10.5 48.1 %copy-start.9 = (bf16[64,128]{1,0:T(8,128)(2,1)S(1)}, bf16[64,128]{1,0:T(8,128)(2,1)}, u32[]{:S(2)}) copy-start(bf16[64,128]{1,0:T(8,128)(2,1)} %param.15) | copy-start | bytes 49156
  11.4 52.4 %copy-start.5 = (bf16[1,512,896]{2,1,0:T(8,128)(2,1)S(1)}, bf16[1,512,896]{2,1,0:T(8,128)(2,1)}, u32[]{:S(2)}) copy-start(bf16[1,512,896]{2,1,0:T(8,128)(2,1)} %param.23) | copy-start | bytes 2752516
  14.8 98.5 %all-to-all-start = ((bf16[16,24,896]{2,1,0:T(8,128)(2,1)}), bf16[16,24,896]{2,1,0:T(8,128)(2,1)S(1)}, u32[]{:S(2)}, u32[]{:S(2)}) async-start(bf16[16,24,896]{2,1,0:T(8,128)(2,1)} %bitcast.2), calls=%async_computation | async-start | bytes 1376256 | tf_op jit(solution)/shard_map/go_a/all_to_all | solution.py:74
  58.5 52.0 %all-gather.2.cloned.1.call-start = ((), (), s32[]{:S(2)}) async-start(), calls=%async_computation.6 | async-start | bytes 1327104 | tf_op jit(solution)/shard_map/all_gather | solution.py:18
  59.3 10.0 %copy-start.6 = (bf16[1,896,512]{2,1,0:T(8,128)(2,1)S(1)}, bf16[1,896,512]{2,1,0:T(8,128)(2,1)}, u32[]{:S(2)}) copy-start(bf16[1,896,512]{2,1,0:T(8,128)(2,1)} %param.22) | copy-start | bytes 2752516
  59.3 11.1 %collective-permute-start = (bf16[896,512]{1,0:T(8,128)(2,1)}, bf16[896,512]{1,0:T(8,128)(2,1)S(1)}, u32[]{:S(2)}, u32[]{:S(2)}) collective-permute-start(bf16[896,512]{1,0:T(8,128)(2,1)} %bitcast.84), channel_id=1, source_target_pairs={{0,1},{1,0},{2,3},{3,2},{4,5},{5,4},{6,7},{7,6},{8,9},{9,8},{10,11... | collective-permute-start | bytes 2752520 | tf_op jit(solution)/shard_map/ppermute | solution.py:28
  61.4 10.1 %collective-permute-start.1 = (bf16[896,512]{1,0:T(8,128)(2,1)}, bf16[896,512]{1,0:T(8,128)(2,1)S(1)}, u32[]{:S(2)}, u32[]{:S(2)}) collective-permute-start(bf16[896,512]{1,0:T(8,128)(2,1)} %bitcast.85), channel_id=1, source_target_pairs={{0,1},{1,0},{2,3},{3,2},{4,5},{5,4},{6,7},{7,6},{8,9},{9,8},{10,11... | collective-permute-start | bytes 2752520 | tf_op jit(solution)/shard_map/ppermute | solution.py:28
  63.8 9.4 %collective-permute-start.2 = (bf16[512,896]{1,0:T(8,128)(2,1)S(1)}, bf16[512,896]{1,0:T(8,128)(2,1)S(1)}, u32[]{:S(2)}, u32[]{:S(2)}) collective-permute-start(bf16[512,896]{1,0:T(8,128)(2,1)S(1)} %bitcast.82), channel_id=1, source_target_pairs={{0,1},{1,0},{2,3},{3,2},{4,5},{5,4},{6,7},{7,6},{8,9},{9,8},{10,11... | collective-permute-start | bytes 2752520 | tf_op jit(solution)/shard_map/ppermute | solution.py:28
  74.7 52.0 %copy-start.10 = (f32[896]{0:T(1024)S(1)}, f32[896]{0:T(1024)}, u32[]{:S(2)}) copy-start(f32[896]{0:T(1024)} %param.18) | copy-start | bytes 10756
  113.5 43.8 %all-to-all-start.2 = ((bf16[16,24,896]{2,1,0:T(8,128)(2,1)}), bf16[16,24,896]{2,1,0:T(8,128)(2,1)S(1)}, u32[]{:S(2)}, u32[]{:S(2)}) async-start(bf16[16,24,896]{2,1,0:T(8,128)(2,1)} %bitcast.79), calls=%async_computation.3 | async-start | bytes 1376256 | tf_op jit(solution)/shard_map/go_b/all_to_all | solution.py:74
  126.6 50.9 %reduce-scatter.3.cloned.1.call-start = ((), (), s32[]{:S(2)}) async-start(), calls=%async_computation.7 | async-start | bytes 1880064 | tf_op jit(solution)/shard_map/sum_a/reduce_scatter | solution.py:91
  132.0 95.3 %reduce-scatter.5.cloned.1.call-start = ((), (), s32[]{:S(2)}) async-start(), calls=%async_computation.8 | async-start | bytes 1880064 | tf_op jit(solution)/shard_map/sum_b/reduce_scatter | solution.py:91
  163.1 42.4 %copy-start.1 = (bf16[1024,896]{1,0:T(8,128)(2,1)S(1)}, bf16[1024,896]{1,0:T(8,128)(2,1)}, u32[]{:S(2)}) copy-start(bf16[1024,896]{1,0:T(8,128)(2,1)} %pad_maximum_fusion) | copy-start | bytes 5505028
  207.4 49.7 %all-to-all-start.1 = ((bf16[16,24,896]{2,1,0:T(8,128)(2,1)}), bf16[16,24,896]{2,1,0:T(8,128)(2,1)S(1)}, u32[]{:S(2)}, u32[]{:S(2)}) async-start(bf16[16,24,896]{2,1,0:T(8,128)(2,1)} %bitcast.87), calls=%async_computation.2 | async-start | bytes 1376256 | tf_op jit(solution)/shard_map/back_a/all_to_all | solution.py:74
  227.4 27.9 %copy-start.2 = (bf16[1024,896]{1,0:T(8,128)(2,1)S(1)}, bf16[1024,896]{1,0:T(8,128)(2,1)}, u32[]{:S(2)}) copy-start(bf16[1024,896]{1,0:T(8,128)(2,1)} %pad_maximum_fusion) | copy-start | bytes 5505028
  255.2 15.5 %copy-start.7 = (bf16[128,2048]{1,0:T(8,128)(2,1)S(1)}, bf16[128,2048]{1,0:T(8,128)(2,1)}, u32[]{:S(2)}) copy-start(bf16[128,2048]{1,0:T(8,128)(2,1)} %param.12) | copy-start | bytes 1572868
  257.1 38.7 %all-to-all-start.3 = ((bf16[16,24,896]{2,1,0:T(8,128)(2,1)}), bf16[16,24,896]{2,1,0:T(8,128)(2,1)S(1)}, u32[]{:S(2)}, u32[]{:S(2)}) async-start(bf16[16,24,896]{2,1,0:T(8,128)(2,1)} %bitcast.86), calls=%async_computation.5 | async-start | bytes 1376256 | tf_op jit(solution)/shard_map/back_b/all_to_all | solution.py:74
  279.1 2.5 copy-start.4
Sparse Core Ops, SparseCore 0:
  61.9 48.4 all-gather.1
  132.1 45.2 reduce-scatter.2
  180.4 46.9 reduce-scatter.4

commit v3 on v2

--- a/solution.py
+++ b/solution.py
@@ -66,10 +66,6 @@
     return attn_heads.reshape(seq_rows, head_count * w_uv.shape[2]).astype(jnp.bfloat16)
 
 
-def sent_rows(route_map, tokens):
-    return jnp.dot(route_map.T, tokens, preferred_element_type=jnp.float32).astype(jnp.bfloat16)
-
-
 def to_same_core(rows, count):
     return lax.all_to_all(
         rows.reshape(count, -1, rows.shape[1]),
@@ -87,7 +83,10 @@
     gained = (rows_wide * norm_gain[None, :]).astype(jnp.bfloat16)
     in_part = jnp.dot(gained, in_w, preferred_element_type=jnp.float32)
     column = lax.broadcasted_iota(jnp.int32, in_part.shape, 1)
-    in_part = jnp.where(column < in_w.shape[1] - lanes, in_part, row_sq).astype(jnp.bfloat16)
+    return jnp.where(column < in_w.shape[1] - lanes, in_part, row_sq).astype(jnp.bfloat16)
+
+
+def row_shares(in_part):
     return lax.psum_scatter(in_part, "ctx", scatter_dimension=0, tiled=True)
 
 
@@ -119,7 +118,6 @@
     w_up,
     w_down,
 ):
-    lat_piece, rope_piece = in_one_piece((latent_keys, rope_keys), "ctx", 1, 0)
     model_width = moe_tokens.shape[1] * lax.axis_size("ctx")
     half_width = w_gate.shape[2]
 
@@ -127,25 +125,37 @@
     expert_count = lax.axis_size("ep") // 2
     capacity = min(tok_rows, 3 * tok_rows * top_count // (2 * expert_count))
     chunk = capacity // 2
-    chunk_rows = expert_count * chunk
-    flat_ids = expert_ids.reshape(-1)
-    onehot = (flat_ids[:, None] == jnp.arange(expert_count, dtype=jnp.int32)[None, :]).astype(
-        jnp.int32
-    )
-    slot_index = jnp.sum((jnp.cumsum(onehot, axis=0) - onehot) * onehot, axis=1)
-    target_slot = (slot_index // chunk) * chunk_rows + flat_ids * chunk + slot_index % chunk
-    place_map = (
-        target_slot[:, None] == jnp.arange(2 * chunk_rows, dtype=jnp.int32)[None, :]
-    ).astype(jnp.float32)
-    place_map = place_map.reshape(tok_rows, top_count, 2 * chunk_rows)
-    route_map = jnp.sum(place_map, axis=1).astype(jnp.bfloat16)
-    weight_map = jnp.sum(place_map * route_scale[:, :, None], axis=1)
-    weight_high = weight_map.astype(jnp.bfloat16)
-    weight_low = (weight_map - weight_high.astype(jnp.float32)).astype(jnp.bfloat16)
-
-    with jax.named_scope("go_a"):
-        rows_a = to_same_core(sent_rows(route_map[:, :chunk_rows], moe_tokens), expert_count)
-    send_b = sent_rows(route_map[:, chunk_rows:], moe_tokens)
+    expert = jnp.arange(expert_count, dtype=jnp.int32)[:, None]
+    hits = [expert == expert_ids[:, k][None, :] for k in range(top_count)]
+    member = sum(hit.astype(jnp.float32) for hit in hits)
+    expert_weight = sum(
+        jnp.where(hit, route_scale[:, k][None, :], 0.0) for k, hit in enumerate(hits)
+    )
+    token = jnp.arange(tok_rows, dtype=jnp.int32)
+    earlier = (token[:, None] < token[None, :]).astype(jnp.bfloat16)
+    slot = jnp.dot(member.astype(jnp.bfloat16), earlier, preferred_element_type=jnp.float32)
+    slot = jnp.where(member > 0.0, slot, -1.0)
+
+    def placed(at):
+        wanted = jnp.arange(at * chunk, (at + 1) * chunk, dtype=jnp.int32).astype(jnp.float32)
+        return slot[:, None, :] == wanted[None, :, None]
+
+    def sent_rows(at):
+        route_map = placed(at).astype(jnp.bfloat16).reshape(expert_count * chunk, tok_rows)
+        return jnp.dot(route_map, moe_tokens, preferred_element_type=jnp.float32).astype(jnp.bfloat16)
+
+    def weighted_sum(at, back):
+        weights = jnp.where(placed(at), expert_weight[:, None, :], 0.0)
+        weights = weights.reshape(expert_count * chunk, tok_rows)
+        high = weights.astype(jnp.bfloat16)
+        low = (weights - high.astype(jnp.float32)).astype(jnp.bfloat16)
+        return sum(
+            lax.dot_general(part, back, (((0,), (0,)), ((), ())), preferred_element_type=jnp.float32)
+            for part in (high, low)
+        )
+
+    rows_a = to_same_core(sent_rows(0), expert_count)
+    send_b = sent_rows(1)
     in_w = jnp.concatenate(
         [
             w_gate[0],
@@ -157,35 +167,23 @@
         axis=1,
     )
     down_w = jnp.concatenate([w_down[0], of_other_core(w_down[0], "ep")], axis=0)
-    rows_a, send_b, in_w, down_w, lat_piece, rope_piece = lax.optimization_barrier(
-        (rows_a, send_b, in_w, down_w, lat_piece, rope_piece)
-    )
-    with jax.named_scope("go_b"):
-        rows_b = to_same_core(send_b, expert_count)
-    with jax.named_scope("sum_a"):
-        share_a = activation_sums(rows_a, norm_gain, in_w)
+    rows_a, send_b, in_w, down_w = lax.optimization_barrier((rows_a, send_b, in_w, down_w))
+    part_a = activation_sums(rows_a, norm_gain, in_w)
+    part_a, send_b = lax.optimization_barrier((part_a, send_b))
+    share_a = row_shares(part_a)
+    rows_b = to_same_core(send_b, expert_count)
+    share_b = row_shares(activation_sums(rows_b, norm_gain, in_w))
+    share_b, latent_keys, rope_keys = lax.optimization_barrier((share_b, latent_keys, rope_keys))
+    lat_piece, rope_piece = in_one_piece((latent_keys, rope_keys), "ctx", 1, 0)
     attn_out = attention(q_latent, q_rope, lat_piece, rope_piece, w_uv)
-    with jax.named_scope("sum_b"):
-        share_b = activation_sums(rows_b, norm_gain, in_w)
-    with jax.named_scope("act_a"):
-        hidden_a = activations(share_a, model_width, half_width)
-    with jax.named_scope("down_a"):
-        out_a = jnp.dot(hidden_a, down_w, preferred_element_type=jnp.float32).astype(jnp.bfloat16)
-    with jax.named_scope("back_a"):
-        back_a = to_same_core(out_a, expert_count)
-    with jax.named_scope("act_b"):
-        hidden_b = activations(share_b, model_width, half_width)
-    with jax.named_scope("down_b"):
-        out_b = jnp.dot(hidden_b, down_w, preferred_element_type=jnp.float32).astype(jnp.bfloat16)
-    with jax.named_scope("back_b"):
-        back_b = to_same_core(out_b, expert_count)
-    moe_out = jnp.zeros((tok_rows, moe_tokens.shape[1]), jnp.float32)
-    for at, back in ((0, back_a), (chunk_rows, back_b)):
-        for part in (weight_high, weight_low):
-            moe_out = moe_out + jnp.dot(
-                part[:, at : at + chunk_rows], back, preferred_element_type=jnp.float32
-            )
-    return (attn_out, moe_out.astype(jnp.bfloat16))
+    hidden_a = activations(share_a, model_width, half_width)
+    out_a = jnp.dot(hidden_a, down_w, preferred_element_type=jnp.float32).astype(jnp.bfloat16)
+    back_a = to_same_core(out_a, expert_count)
+    hidden_b = activations(share_b, model_width, half_width)
+    out_b = jnp.dot(hidden_b, down_w, preferred_element_type=jnp.float32).astype(jnp.bfloat16)
+    back_b = to_same_core(out_b, expert_count)
+    moe_out = (weighted_sum(0, back_a) + weighted_sum(1, back_b)).astype(jnp.bfloat16)
+    return (attn_out, moe_out)
 
 
 def solution(mesh):

time: 306 us -> 285 us (0.931)
  local copies, waits for them, and re-layouts: 15.3 us -> 6.38 us
  other arithmetic: 12.4 us -> 5.35 us
  starting transfers between devices: 89.3 us -> 84.2 us
    all_to_all x4, waiting for transfers between devices: 39 us -> 72.7 us  [to_same_core(): lax.all_to_all(rows.reshape(count, -1, rows.shape[1]), 'ep', split_axis=0...]
    all_gather x1, waiting for transfers between devices: 35.7 us -> 3.19 us  [in_one_piece(): lax.all_gather(both, axis, axis=dim, tiled=True)]
    all_to_all x4, starting transfers between devices: 82.6 us -> 77.5 us  [to_same_core(): lax.all_to_all(rows.reshape(count, -1, rows.shape[1]), 'ep', split_axis=0...]
    unnamed x30 -> x35, local copies, waits for them, and re-layouts: 9.14 us -> 4.99 us
    dot_general x6 -> x7, matrix products: 6.75 us -> 8.39 us  [the longest x2 4.47 us: sent_rows(): jnp.dot(route_map, moe_tokens, preferred_element_type=jnp.float32)]
  transfers between devices with their start and end apart: 10 -> 10, of which waited for: 5 -> 6; matrix products, arithmetic and copies ran while one was open for 14% -> 8% of each run, Pallas kernels for 0% -> 0%
where the time goes in v3:
time: 285 us; the launch traced here: 284 us
  waiting for transfers between devices  95 us (33%)
  starting transfers between devices  84.2 us (30%)
  blocking collectives  53.2 us (19%)
  matrix products  26.3 us (9%)
  between operations  14.2 us (5%)
  local copies, waits for them, and re-layouts  6.38 us (2%)
  other arithmetic  5.35 us (2%)
    all_to_all x4, starting transfers between devices, to_same_core(): lax.all_to_all(rows.reshape(count, -1, rows.shape[1]), 'ep', split_axis=0...  77.5 us
    all_to_all x4, waiting for transfers between devices, to_same_core(): lax.all_to_all(rows.reshape(count, -1, rows.shape[1]), 'ep', split_axis=0...  72.7 us
    all_gather x2, blocking collectives, activations(): return lax.all_gather(part_hidden, 'ctx', axis=0, tiled=True)  53.2 us
    reduce_scatter x2, waiting for transfers between devices, row_shares(): return lax.psum_scatter(in_part, 'ctx', scatter_dimension=0, tiled=True)  18.2 us
    dot_general x2, matrix products, activation_sums(): in_part = jnp.dot(gained, in_w, preferred_element_type=jnp.float32)  10.7 us
    ppermute x3, starting transfers between devices, of_other_core(): return lax.ppermute(value, axis, [(i, i ^ 1) for i in range(count)])  6.47 us
  transfers between devices with their start and end apart: 10, of which 6 were waited for; matrix products, arithmetic and copies ran while one was open for 8% of the time, Pallas kernels for 0%

profile of v3, /device:TPU:66, one launch (start us, length us, event | category | flops | bytes accessed | tf_op | source)
XLA Modules:
  0.0 284.5 jit_solution(5594488416484230992)
XLA Ops:
  9.2 2.3 convolution_convert_fusion.3
  11.6 43.7 %all-to-all-start = ((bf16[16,24,896]{2,1,0:T(8,128)(2,1)}), bf16[16,24,896]{2,1,0:T(8,128)(2,1)S(1)}, u32[]{:S(2)}, u32[]{:S(2)}) async-start(bf16[16,24,896]{2,1,0:T(8,128)(2,1)} %bitcast.4), calls=%async_computation | async-start | bytes 1376256 | tf_op jit(solution)/shard_map/all_to_all | solution.py:70
  55.3 2.1 collective-permute-start
  57.4 2.4 collective-permute-start.1
  59.8 2.0 collective-permute-start.2
  61.9 2.1 convolution_convert_fusion.2
  64.3 1.8 copy-done.6
  66.3 23.8 %all-to-all-done = bf16[16,24,896]{2,1,0:T(8,128)(2,1)S(1)} async-done(((bf16[16,24,896]{2,1,0:T(8,128)(2,1)}), bf16[16,24,896]{2,1,0:T(8,128)(2,1)S(1)}, u32[]{:S(2)}, u32[]{:S(2)}) %all-to-all-start) | async-done | bytes 688160 | tf_op jit(solution)/shard_map/all_to_all | solution.py:70
  90.3 5.3 %fusion = bf16[384,2176]{1,0:T(8,128)(2,1)} fusion(bf16[896,2176]{1,0:T(8,128)(2,1)} %copy-done.6, bf16[384]{0:T(512)(128)(2,1)S(1)} %fusion.5, pred[2176]{0:T(1024)(128)(4,1)S(1)} %iota_compare_fusion.5, bf16[384,896]{1,0:T(8,128)(2,1)S(1)} %bitcast.75, f32[896]{0:T(1024)S(1)} %copy-done.11), kind=kOutput, calls=%fused_computation.2 | convolution fusion | flops 1499234304 | bytes 6265216 | tf_op jit(solution)/shard_map/dot_general | solution.py:84
  95.6 7.7 %all-to-all-start.1 = ((bf16[16,24,896]{2,1,0:T(8,128)(2,1)}), bf16[16,24,896]{2,1,0:T(8,128)(2,1)S(1)}, u32[]{:S(2)}, u32[]{:S(2)}) async-start(bf16[16,24,896]{2,1,0:T(8,128)(2,1)} %bitcast.9), calls=%async_computation.1 | async-start | bytes 1376256 | tf_op jit(solution)/shard_map/all_to_all | solution.py:70
  104.1 34.1 %all-to-all-done.1 = bf16[16,24,896]{2,1,0:T(8,128)(2,1)S(1)} async-done(((bf16[16,24,896]{2,1,0:T(8,128)(2,1)}), bf16[16,24,896]{2,1,0:T(8,128)(2,1)S(1)}, u32[]{:S(2)}, u32[]{:S(2)}) %all-to-all-start.1) | async-done | bytes 688160 | tf_op jit(solution)/shard_map/all_to_all | solution.py:70
  138.7 5.4 %fusion.1 = bf16[384,2176]{1,0:T(8,128)(2,1)} fusion(bf16[384,896]{1,0:T(8,128)(2,1)S(1)} %fusion.6, bf16[896,2176]{1,0:T(8,128)(2,1)} %copy-done.6, bf16[384]{0:T(512)(128)(2,1)S(1)} %broadcast_in_dim.89, pred[2176]{0:T(1024)(128)(4,1)S(1)} %iota_compare_fusion.5), kind=kOutput, calls=%fused_computation.3 | convolution fusion | flops 1498202112 | bytes 6261632 | tf_op jit(solution)/shard_map/dot_general | solution.py:84
  144.1 11.6 %reduce-scatter.5.cloned.1.call-done = bf16[48,2176]{1,0:T(8,128)(2,1)} async-done(((bf16[384,2176]{1,0:T(8,128)(2,1)}), bf16[48,2176]{1,0:T(8,128)(2,1)}) %reduce-scatter.5.cloned.1.call-update) | async-done | bytes 208912 | tf_op jit(solution)/shard_map/reduce_scatter | solution.py:90
  157.1 26.8 %all_gather.10 = bf16[384,1024]{1,0:T(8,128)(2,1)S(1)} all-gather(bf16[48,1024]{1,0:T(8,128)(2,1)S(1)} %pad_maximum_fusion.2), channel_id=1, replica_groups=mesh['group'=2,'ctx'=8,'ep'=32] {'ctx'}, dimensions={0}, use_global_device_ids=true | all-gather | bytes 884736 | tf_op jit(solution)/shard_map/all_gather | solution.py:104
  183.9 1.8 convolution_convert_fusion.1
  185.8 12.9 %all-to-all-start.2 = ((bf16[16,24,896]{2,1,0:T(8,128)(2,1)}), bf16[16,24,896]{2,1,0:T(8,128)(2,1)S(1)}, u32[]{:S(2)}, u32[]{:S(2)}) async-start(bf16[16,24,896]{2,1,0:T(8,128)(2,1)} %bitcast.82), calls=%async_computation.4 | async-start | bytes 1376256 | tf_op jit(solution)/shard_map/all_to_all | solution.py:70
  198.8 6.6 %reduce-scatter.3.cloned.1.call-done = bf16[48,2176]{1,0:T(8,128)(2,1)} async-done(((bf16[384,2176]{1,0:T(8,128)(2,1)}), bf16[48,2176]{1,0:T(8,128)(2,1)}) %reduce-scatter.3.cloned.1.call-update) | async-done | bytes 208912 | tf_op jit(solution)/shard_map/reduce_scatter | solution.py:90
  207.5 26.4 %all_gather.11 = bf16[384,1024]{1,0:T(8,128)(2,1)S(1)} all-gather(bf16[48,1024]{1,0:T(8,128)(2,1)S(1)} %pad_maximum_fusion.3), channel_id=1, replica_groups=mesh['group'=2,'ctx'=8,'ep'=32] {'ctx'}, dimensions={0}, use_global_device_ids=true | all-gather | bytes 884736 | tf_op jit(solution)/shard_map/all_gather | solution.py:104
  233.9 1.8 convolution_convert_fusion
  235.7 13.2 %all-to-all-start.3 = ((bf16[16,24,896]{2,1,0:T(8,128)(2,1)}), bf16[16,24,896]{2,1,0:T(8,128)(2,1)S(1)}, u32[]{:S(2)}, u32[]{:S(2)}) async-start(bf16[16,24,896]{2,1,0:T(8,128)(2,1)} %bitcast.81), calls=%async_computation.5 | async-start | bytes 1376256 | tf_op jit(solution)/shard_map/all_to_all | solution.py:70
  250.7 1.5 convolution_bitcast_fusion.2
  252.1 3.2 %all-gather.2.cloned.1.call-done = bf16[576,1024]{1,0:T(8,128)(2,1)} async-done(((bf16[576,128]{1,0:T(8,128)(2,1)}), bf16[576,1024]{1,0:T(8,128)(2,1)}) %all-gather.2.cloned.1.call-update) | async-done | bytes 1179664 | tf_op jit(solution)/shard_map/all_gather | solution.py:18
  255.3 1.5 fusion.40
  260.2 14.8 %all-to-all-done.3 = bf16[16,24,896]{2,1,0:T(8,128)(2,1)S(1)} async-done(((bf16[16,24,896]{2,1,0:T(8,128)(2,1)}), bf16[16,24,896]{2,1,0:T(8,128)(2,1)S(1)}, u32[]{:S(2)}, u32[]{:S(2)}) %all-to-all-start.3) | async-done | bytes 688160 | tf_op jit(solution)/shard_map/all_to_all | solution.py:70
  (82 shorter events, 15.4 us)
Async XLA Ops:
  7.2 251.8 %copy-start = (bf16[4,512,128]{2,1,0:T(8,128)(2,1)S(1)}, bf16[4,512,128]{2,1,0:T(8,128)(2,1)}, u32[]{:S(2)}) copy-start(bf16[4,512,128]{2,1,0:T(8,128)(2,1)} %param.16) | copy-start | bytes 1572868
  7.2 48.1 %copy-start.4 = (bf16[1,896,512]{2,1,0:T(8,128)(2,1)S(1)}, bf16[1,896,512]{2,1,0:T(8,128)(2,1)}, u32[]{:S(2)}) copy-start(bf16[1,896,512]{2,1,0:T(8,128)(2,1)} %param.21) | copy-start | bytes 2752516
  7.2 52.6 %copy-start.2 = (bf16[1,512,896]{2,1,0:T(8,128)(2,1)S(1)}, bf16[1,512,896]{2,1,0:T(8,128)(2,1)}, u32[]{:S(2)}) copy-start(bf16[1,512,896]{2,1,0:T(8,128)(2,1)} %param.23) | copy-start | bytes 2752516
  9.2 52.6 %copy-start.1 = (bf16[256,896]{1,0:T(8,128)(2,1)S(1)}, bf16[256,896]{1,0:T(8,128)(2,1)}, u32[]{:S(2)}) copy-start(bf16[256,896]{1,0:T(8,128)(2,1)} %param.17) | copy-start | bytes 1376260
  11.6 78.5 %all-to-all-start = ((bf16[16,24,896]{2,1,0:T(8,128)(2,1)}), bf16[16,24,896]{2,1,0:T(8,128)(2,1)S(1)}, u32[]{:S(2)}, u32[]{:S(2)}) async-start(bf16[16,24,896]{2,1,0:T(8,128)(2,1)} %bitcast.4), calls=%async_computation | async-start | bytes 1376256 | tf_op jit(solution)/shard_map/all_to_all | solution.py:70
  55.2 8.8 %copy-start.5 = (bf16[1,896,512]{2,1,0:T(8,128)(2,1)S(1)}, bf16[1,896,512]{2,1,0:T(8,128)(2,1)}, u32[]{:S(2)}) copy-start(bf16[1,896,512]{2,1,0:T(8,128)(2,1)} %param.22) | copy-start | bytes 2752516
  55.3 8.8 %collective-permute-start = (bf16[896,512]{1,0:T(8,128)(2,1)S(1)}, bf16[896,512]{1,0:T(8,128)(2,1)S(1)}, u32[]{:S(2)}, u32[]{:S(2)}) collective-permute-start(bf16[896,512]{1,0:T(8,128)(2,1)S(1)} %bitcast.79), channel_id=1, source_target_pairs={{0,1},{1,0},{2,3},{3,2},{4,5},{5,4},{6,7},{7,6},{8,9},{9,8},{10,11... | collective-permute-start | bytes 2752520 | tf_op jit(solution)/shard_map/ppermute | solution.py:28
  57.4 6.8 %collective-permute-start.1 = (bf16[896,512]{1,0:T(8,128)(2,1)}, bf16[896,512]{1,0:T(8,128)(2,1)S(1)}, u32[]{:S(2)}, u32[]{:S(2)}) collective-permute-start(bf16[896,512]{1,0:T(8,128)(2,1)} %bitcast.80), channel_id=1, source_target_pairs={{0,1},{1,0},{2,3},{3,2},{4,5},{5,4},{6,7},{7,6},{8,9},{9,8},{10,11... | collective-permute-start | bytes 2752520 | tf_op jit(solution)/shard_map/ppermute | solution.py:28
  59.8 6.3 %collective-permute-start.2 = (bf16[512,896]{1,0:T(8,128)(2,1)S(1)}, bf16[512,896]{1,0:T(8,128)(2,1)S(1)}, u32[]{:S(2)}, u32[]{:S(2)}) collective-permute-start(bf16[512,896]{1,0:T(8,128)(2,1)S(1)} %bitcast.77), channel_id=1, source_target_pairs={{0,1},{1,0},{2,3},{3,2},{4,5},{5,4},{6,7},{7,6},{8,9},{9,8},{10,11... | collective-permute-start | bytes 2752520 | tf_op jit(solution)/shard_map/ppermute | solution.py:28
  64.1 2.1 copy-start.3
  64.3 1.8 copy-start.6
  66.1 24.1 %copy-start.11 = (f32[896]{0:T(1024)S(1)}, f32[896]{0:T(1024)}, u32[]{:S(2)}) copy-start(f32[896]{0:T(1024)} %param.18) | copy-start | bytes 10756
  95.6 42.7 %all-to-all-start.1 = ((bf16[16,24,896]{2,1,0:T(8,128)(2,1)}), bf16[16,24,896]{2,1,0:T(8,128)(2,1)S(1)}, u32[]{:S(2)}, u32[]{:S(2)}) async-start(bf16[16,24,896]{2,1,0:T(8,128)(2,1)} %bitcast.9), calls=%async_computation.1 | async-start | bytes 1376256 | tf_op jit(solution)/shard_map/all_to_all | solution.py:70
  103.3 52.5 %reduce-scatter.5.cloned.1.call-start = ((), (), s32[]{:S(2)}) async-start(), calls=%async_computation.8 | async-start | bytes 1880064 | tf_op jit(solution)/shard_map/reduce_scatter | solution.py:90
  104.1 101.4 %reduce-scatter.3.cloned.1.call-start = ((), (), s32[]{:S(2)}) async-start(), calls=%async_computation.6 | async-start | bytes 1880064 | tf_op jit(solution)/shard_map/reduce_scatter | solution.py:90
  183.9 21.5 %copy-start.7 = (bf16[512,128]{1,0:T(8,128)(2,1)S(1)}, bf16[512,128]{1,0:T(8,128)(2,1)}, u32[]{:S(2)}) copy-start(bf16[512,128]{1,0:T(8,128)(2,1)} %param.14) | copy-start | bytes 393220
  183.9 21.5 %copy-start.9 = (bf16[64,128]{1,0:T(8,128)(2,1)S(1)}, bf16[64,128]{1,0:T(8,128)(2,1)}, u32[]{:S(2)}) copy-start(bf16[64,128]{1,0:T(8,128)(2,1)} %param.15) | copy-start | bytes 49156
  185.8 49.9 %all-to-all-start.2 = ((bf16[16,24,896]{2,1,0:T(8,128)(2,1)}), bf16[16,24,896]{2,1,0:T(8,128)(2,1)S(1)}, u32[]{:S(2)}, u32[]{:S(2)}) async-start(bf16[16,24,896]{2,1,0:T(8,128)(2,1)} %bitcast.82), calls=%async_computation.4 | async-start | bytes 1376256 | tf_op jit(solution)/shard_map/all_to_all | solution.py:70
  198.7 56.6 %all-gather.2.cloned.1.call-start = ((), (), s32[]{:S(2)}) async-start(), calls=%async_computation.7 | async-start | bytes 1327104 | tf_op jit(solution)/shard_map/all_gather | solution.py:18
  233.9 15.1 %copy-start.8 = (bf16[128,256]{1,0:T(8,128)(2,1)S(1)}, bf16[128,256]{1,0:T(8,128)(2,1)}, u32[]{:S(2)}) copy-start(bf16[128,256]{1,0:T(8,128)(2,1)} %param.13) | copy-start | bytes 196612
  235.7 14.9 %copy-start.12 = (f32[256,2]{0,1:T(2,128)S(1)}, f32[256,2]{0,1:T(2,128)}, u32[]{:S(2)}) copy-start(f32[256,2]{0,1:T(2,128)} %param.20) | copy-start | bytes 6148
  235.7 39.3 %all-to-all-start.3 = ((bf16[16,24,896]{2,1,0:T(8,128)(2,1)}), bf16[16,24,896]{2,1,0:T(8,128)(2,1)S(1)}, u32[]{:S(2)}, u32[]{:S(2)}) async-start(bf16[16,24,896]{2,1,0:T(8,128)(2,1)} %bitcast.81), calls=%async_computation.5 | async-start | bytes 1376256 | tf_op jit(solution)/shard_map/all_to_all | solution.py:70
  255.3 1.5 copy-start.10
  275.5 1.2 copy-start.13
Sparse Core Ops, SparseCore 0:
  107.0 48.7 reduce-scatter.4
  158.6 46.7 reduce-scatter.2
  208.0 47.2 all-gather.1

commit v4 on v3

--- a/solution.py
+++ b/solution.py
@@ -1,6 +1,8 @@
 import jax
 import jax.numpy as jnp
 from jax import lax
+from jax.experimental import pallas as pl
+from jax.experimental.pallas import tpu as pltpu
 from jax.sharding import PartitionSpec as P
 
 score_scale = 192.0 ** (-0.5)
@@ -77,13 +79,63 @@
     ).reshape(rows.shape)
 
 
-def activation_sums(rows, norm_gain, in_w):
-    rows_wide = rows.astype(jnp.float32)
+def sums_kernel(rows, gain, *refs):
+    count = len(refs) - 6
+    weights, out = refs[:count], refs[count]
+    gained, fetched, sums, fetch_done, store_done = refs[count + 1 :]
+    width = fetched.shape[2]
+    fetches = [
+        pltpu.make_async_copy(weights[i], fetched.at[i], fetch_done.at[i]) for i in range(count)
+    ]
+    for fetch in fetches:
+        fetch.start()
+    rows_wide = rows[...].astype(jnp.float32)
+    gained[...] = (rows_wide * gain[...]).astype(jnp.bfloat16)
     row_sq = jnp.sum(rows_wide * rows_wide, axis=1, keepdims=True)
-    gained = (rows_wide * norm_gain[None, :]).astype(jnp.bfloat16)
-    in_part = jnp.dot(gained, in_w, preferred_element_type=jnp.float32)
-    column = lax.broadcasted_iota(jnp.int32, in_part.shape, 1)
-    return jnp.where(column < in_w.shape[1] - lanes, in_part, row_sq).astype(jnp.bfloat16)
+    sums[:, count * width :] = jnp.broadcast_to(row_sq, (rows.shape[0], lanes)).astype(jnp.bfloat16)
+    ends = [(i + 1) * width for i in range(count - 1)] + [sums.shape[1]]
+    stores = []
+    for i in range(count):
+        fetches[i].wait()
+        sums[:, i * width : (i + 1) * width] = jnp.dot(
+            gained[...], fetched[i], preferred_element_type=jnp.float32
+        ).astype(jnp.bfloat16)
+        piece = pl.ds(i * width, ends[i] - i * width)
+        store = pltpu.make_async_copy(sums.at[:, piece], out.at[:, piece], store_done.at[i])
+        store.start()
+        stores.append(store)
+    for store in stores:
+        store.wait()
+
+
+def activation_sums(rows, norm_gain, weights):
+    row_count, width = rows.shape
+    block = weights[0].shape[1]
+    count = len(weights)
+    columns = count * block + lanes
+    return pl.pallas_call(
+        sums_kernel,
+        out_shape=jax.ShapeDtypeStruct((row_count, columns), jnp.bfloat16),
+        in_specs=[
+            pl.BlockSpec(memory_space=pltpu.VMEM),
+            pl.BlockSpec(memory_space=pltpu.VMEM),
+            *[pl.BlockSpec(memory_space=pl.ANY) for _ in weights],
+        ],
+        out_specs=pl.BlockSpec(memory_space=pl.ANY),
+        scratch_shapes=[
+            pltpu.VMEM((row_count, width), jnp.bfloat16),
+            pltpu.VMEM((count, width, block), jnp.bfloat16),
+            pltpu.VMEM((row_count, columns), jnp.bfloat16),
+            pltpu.SemaphoreType.DMA((count,)),
+            pltpu.SemaphoreType.DMA((count,)),
+        ],
+        cost_estimate=pl.CostEstimate(
+            flops=2 * row_count * width * count * block,
+            bytes_accessed=2 * (row_count * (width + columns) + count * width * block),
+            transcendentals=0,
+        ),
+        name="gate_up_sums",
+    )(rows, norm_gain[None, :], *weights)
 
 
 def row_shares(in_part):
@@ -118,6 +170,7 @@
     w_up,
     w_down,
 ):
+    lat_piece, rope_piece = in_one_piece((latent_keys, rope_keys), "ctx", 1, 0)
     model_width = moe_tokens.shape[1] * lax.axis_size("ctx")
     half_width = w_gate.shape[2]
 
@@ -156,16 +209,7 @@
 
     rows_a = to_same_core(sent_rows(0), expert_count)
     send_b = sent_rows(1)
-    in_w = jnp.concatenate(
-        [
-            w_gate[0],
-            w_up[0],
-            of_other_core(w_gate[0], "ep"),
-            of_other_core(w_up[0], "ep"),
-            jnp.zeros((w_gate.shape[1], lanes), jnp.bfloat16),
-        ],
-        axis=1,
-    )
+    in_w = (w_gate[0], w_up[0], of_other_core(w_gate[0], "ep"), of_other_core(w_up[0], "ep"))
     down_w = jnp.concatenate([w_down[0], of_other_core(w_down[0], "ep")], axis=0)
     rows_a, send_b, in_w, down_w = lax.optimization_barrier((rows_a, send_b, in_w, down_w))
     part_a = activation_sums(rows_a, norm_gain, in_w)
@@ -173,8 +217,6 @@
     share_a = row_shares(part_a)
     rows_b = to_same_core(send_b, expert_count)
     share_b = row_shares(activation_sums(rows_b, norm_gain, in_w))
-    share_b, latent_keys, rope_keys = lax.optimization_barrier((share_b, latent_keys, rope_keys))
-    lat_piece, rope_piece = in_one_piece((latent_keys, rope_keys), "ctx", 1, 0)
     attn_out = attention(q_latent, q_rope, lat_piece, rope_piece, w_uv)
     hidden_a = activations(share_a, model_width, half_width)
     out_a = jnp.dot(hidden_a, down_w, preferred_element_type=jnp.float32).astype(jnp.bfloat16)

time: 285 us -> 269 us (0.944)
  the two profiles are of different devices: /device:TPU:66 before, /device:TPU:68 now
where the time goes in v4:
time: 269 us; the launch traced here: 268 us
  blocking collectives  101 us (38%)
  starting transfers between devices  67.3 us (25%)
  waiting for transfers between devices  48.8 us (18%)
  matrix products  14.7 us (5%)
  between operations  14.2 us (5%)
  Pallas kernels  11 us (4%)
  other arithmetic  6.73 us (3%)
  local copies, waits for them, and re-layouts  5.04 us (2%)
    all_to_all x3, starting transfers between devices, to_same_core(): lax.all_to_all(rows.reshape(count, -1, rows.shape[1]), 'ep', split_axis=0...  60.7 us
    all_gather x2, blocking collectives, activations(): return lax.all_gather(part_hidden, 'ctx', axis=0, tiled=True)  55.3 us
    all_to_all x1, blocking collectives, to_same_core(): lax.all_to_all(rows.reshape(count, -1, rows.shape[1]), 'ep', split_axis=0...  45.2 us
    all_to_all x3, waiting for transfers between devices, to_same_core(): lax.all_to_all(rows.reshape(count, -1, rows.shape[1]), 'ep', split_axis=0...  37.8 us
    pallas_call x2, Pallas kernels, activation_sums(): pl.pallas_call(sums_kernel, out_shape=jax.ShapeDtypeStruct((row_count, co...  11 us
    ppermute x3, starting transfers between devices, of_other_core(): return lax.ppermute(value, axis, [(i, i ^ 1) for i in range(count)])  6.34 us
    all_gather x1, waiting for transfers between devices, in_one_piece(): lax.all_gather(both, axis, axis=dim, tiled=True)  5.84 us
  transfers between devices with their start and end apart: 9, of which 4 were waited for; matrix products, arithmetic and copies ran while one was open for 7% of the time, Pallas kernels for 2%

profile of v4, /device:TPU:68, one launch (start us, length us, event | category | flops | bytes accessed | tf_op | source)
XLA Modules:
  0.0 268.2 jit_solution(1845347285251377397)
XLA Ops:
  8.6 2.3 convolution_convert_fusion.3
  10.9 43.7 %all-to-all-start = ((bf16[16,24,896]{2,1,0:T(8,128)(2,1)}), bf16[16,24,896]{2,1,0:T(8,128)(2,1)}, u32[]{:S(2)}, u32[]{:S(2)}) async-start(bf16[16,24,896]{2,1,0:T(8,128)(2,1)} %bitcast.15), calls=%async_computation | async-start | bytes 1376256 | tf_op jit(solution)/shard_map/all_to_all | solution.py:72
  54.7 2.0 collective-permute-start.2
  56.6 2.4 collective-permute-start
  59.1 2.0 collective-permute-start.1
  61.6 2.3 convolution_convert_fusion.2
  63.9 2.6 pad_maximum_fusion
  66.5 23.0 %all-to-all-done = bf16[16,24,896]{2,1,0:T(8,128)(2,1)} async-done(((bf16[16,24,896]{2,1,0:T(8,128)(2,1)}), bf16[16,24,896]{2,1,0:T(8,128)(2,1)}, u32[]{:S(2)}, u32[]{:S(2)}) %all-to-all-start) | async-done | bytes 688160 | tf_op jit(solution)/shard_map/all_to_all | solution.py:72
  89.5 5.5 %gate_up_sums.2 = bf16[384,2176]{1,0:T(8,128)(2,1)} custom-call(bf16[384,896]{1,0:T(8,128)(2,1)} %bitcast.16.rows, f32[1,896]{1,0:T(1,128)} %broadcast_in_dim.77.gain, bf16[896,512]{1,0:T(8,128)(2,1)} %bitcast.66, bf16[896,512]{1,0:T(8,128)(2,1)} %bitcast.69, bf16[896,512]{1,0:T(8,128)(2,1)} %copy-done.3, bf16[896,512]{1,0:T(8,128)(2,1)} %collective-permute-done.1.refs_3_), custom_call_target="tpu_custom_call" | custom-call | flops 1409286144 | bytes 6029312 | tf_op jit(solution)/shard_map/gate_up_sums/pallas_call | solution.py:116
  96.1 45.2 %all_to_all.20 = bf16[16,24,896]{2,1,0:T(8,128)(2,1)} all-to-all(bf16[16,24,896]{2,1,0:T(8,128)(2,1)S(1)} %bitcast.73), channel_id=1, replica_groups={{0,2,4,6,8,10,12,14,16,18,20,22,24,26,28,30},{1,3,5,7,9,11,13,15,17,19,..., dimensions={0} | all-to-all | bytes 1376256 | tf_op jit(solution)/shard_map/all_to_all | solution.py:72
  141.3 5.5 %gate_up_sums.3 = bf16[384,2176]{1,0:T(8,128)(2,1)} custom-call(bf16[384,896]{1,0:T(8,128)(2,1)} %bitcast.72, f32[1,896]{1,0:T(1,128)} %broadcast_in_dim.77.gain, bf16[896,512]{1,0:T(8,128)(2,1)} %bitcast.67, bf16[896,512]{1,0:T(8,128)(2,1)} %bitcast.70, bf16[896,512]{1,0:T(8,128)(2,1)} %copy-done.3, bf16[896,512]{1,0:T(8,128)(2,1)} %collective-permute-done.1.refs_3_), custom_call_target="tpu_custom_call" | custom-call | flops 1409286144 | bytes 6029312 | tf_op jit(solution)/shard_map/gate_up_sums/pallas_call | solution.py:116
  146.9 1.1 convert_element_type.109
  148.4 28.8 %all_gather.10 = bf16[384,1024]{1,0:T(8,128)(2,1)S(1)} all-gather(bf16[48,1024]{1,0:T(8,128)(2,1)S(1)} %pad_maximum_fusion.2), channel_id=1, replica_groups=mesh['group'=2,'ctx'=8,'ep'=32] {'ctx'}, dimensions={0}, use_global_device_ids=true | all-gather | bytes 884736 | tf_op jit(solution)/shard_map/all_gather | solution.py:156
  177.2 1.8 convolution_convert_fusion.1
  179.0 4.8 %all-to-all-start.1 = ((bf16[16,24,896]{2,1,0:T(8,128)(2,1)}), bf16[16,24,896]{2,1,0:T(8,128)(2,1)S(1)}, u32[]{:S(2)}, u32[]{:S(2)}) async-start(bf16[16,24,896]{2,1,0:T(8,128)(2,1)} %bitcast.76), calls=%async_computation.2 | async-start | bytes 1376256 | tf_op jit(solution)/shard_map/all_to_all | solution.py:72
  184.7 5.0 %reduce-scatter.5.cloned.1.call-done = bf16[48,2176]{1,0:T(8,128)(2,1)} async-done(((bf16[384,2176]{1,0:T(8,128)(2,1)}), bf16[48,2176]{1,0:T(8,128)(2,1)}) %reduce-scatter.5.cloned.1.call-update) | async-done | bytes 208912 | tf_op jit(solution)/shard_map/reduce_scatter | solution.py:142
  191.0 26.5 %all_gather.11 = bf16[384,1024]{1,0:T(8,128)(2,1)S(1)} all-gather(bf16[48,1024]{1,0:T(8,128)(2,1)S(1)} %pad_maximum_fusion.3), channel_id=1, replica_groups=mesh['group'=2,'ctx'=8,'ep'=32] {'ctx'}, dimensions={0}, use_global_device_ids=true | all-gather | bytes 884736 | tf_op jit(solution)/shard_map/all_gather | solution.py:156
  217.5 1.8 convolution_convert_fusion
  219.4 12.2 %all-to-all-start.3 = ((bf16[16,24,896]{2,1,0:T(8,128)(2,1)}), bf16[16,24,896]{2,1,0:T(8,128)(2,1)S(1)}, u32[]{:S(2)}, u32[]{:S(2)}) async-start(bf16[16,24,896]{2,1,0:T(8,128)(2,1)} %bitcast.75), calls=%async_computation.5 | async-start | bytes 1376256 | tf_op jit(solution)/shard_map/all_to_all | solution.py:72
  231.7 1.3 copy.20
  233.3 5.8 %all-gather.2.cloned.1.call-done = bf16[576,1024]{1,0:T(8,128)(2,1)} async-done(((bf16[576,128]{1,0:T(8,128)(2,1)}), bf16[576,1024]{1,0:T(8,128)(2,1)}) %all-gather.2.cloned.1.call-update) | async-done | bytes 1179664 | tf_op jit(solution)/shard_map/all_gather | solution.py:20
  239.2 1.5 fusion.33
  244.6 14.8 %all-to-all-done.3 = bf16[16,24,896]{2,1,0:T(8,128)(2,1)S(1)} async-done(((bf16[16,24,896]{2,1,0:T(8,128)(2,1)}), bf16[16,24,896]{2,1,0:T(8,128)(2,1)S(1)}, u32[]{:S(2)}, u32[]{:S(2)}) %all-to-all-start.3) | async-done | bytes 688160 | tf_op jit(solution)/shard_map/all_to_all | solution.py:72
  260.4 1.3 fusion.6
  (68 shorter events, 10.9 us)
Async XLA Ops:
  7.2 235.7 %copy-start = (bf16[4,512,128]{2,1,0:T(8,128)(2,1)S(1)}, bf16[4,512,128]{2,1,0:T(8,128)(2,1)}, u32[]{:S(2)}) copy-start(bf16[4,512,128]{2,1,0:T(8,128)(2,1)} %param.16) | copy-start | bytes 1572868
  7.2 49.4 %copy-start.1 = (bf16[1,896,512]{2,1,0:T(8,128)(2,1)S(1)}, bf16[1,896,512]{2,1,0:T(8,128)(2,1)}, u32[]{:S(2)}) copy-start(bf16[1,896,512]{2,1,0:T(8,128)(2,1)} %param.21) | copy-start | bytes 2752516
  7.2 51.9 %copy-start.2 = (bf16[1,896,512]{2,1,0:T(8,128)(2,1)S(1)}, bf16[1,896,512]{2,1,0:T(8,128)(2,1)}, u32[]{:S(2)}) copy-start(bf16[1,896,512]{2,1,0:T(8,128)(2,1)} %param.22) | copy-start | bytes 2752516
  7.2 53.8 %copy-start.10 = (f32[896]{0:T(1024)S(1)}, f32[896]{0:T(1024)}, u32[]{:S(2)}) copy-start(f32[896]{0:T(1024)} %param.18) | copy-start | bytes 10756
  10.9 78.6 %all-to-all-start = ((bf16[16,24,896]{2,1,0:T(8,128)(2,1)}), bf16[16,24,896]{2,1,0:T(8,128)(2,1)}, u32[]{:S(2)}, u32[]{:S(2)}) async-start(bf16[16,24,896]{2,1,0:T(8,128)(2,1)} %bitcast.15), calls=%async_computation | async-start | bytes 1376256 | tf_op jit(solution)/shard_map/all_to_all | solution.py:72
  54.6 92.3 %reduce-scatter.3.cloned.1.call-start = ((), (), s32[]{:S(2)}) async-start(), calls=%async_computation.7 | async-start | bytes 1880064 | tf_op jit(solution)/shard_map/reduce_scatter | solution.py:142
  54.7 9.2 %collective-permute-start.2 = (bf16[512,896]{1,0:T(8,128)(2,1)}, bf16[512,896]{1,0:T(8,128)(2,1)S(1)}, u32[]{:S(2)}, u32[]{:S(2)}) collective-permute-start(bf16[512,896]{1,0:T(8,128)(2,1)} %bitcast.19), channel_id=1, source_target_pairs={{0,1},{1,0},{2,3},{3,2},{4,5},{5,4},{6,7},{7,6},{8,9},{9,8},{10,11... | collective-permute-start | bytes 2752520 | tf_op jit(solution)/shard_map/ppermute | solution.py:30
  56.6 9.9 %collective-permute-start = (bf16[896,512]{1,0:T(8,128)(2,1)S(1)}, bf16[896,512]{1,0:T(8,128)(2,1)S(1)}, u32[]{:S(2)}, u32[]{:S(2)}) collective-permute-start(bf16[896,512]{1,0:T(8,128)(2,1)S(1)} %bitcast.68), channel_id=1, source_target_pairs={{0,1},{1,0},{2,3},{3,2},{4,5},{5,4},{6,7},{7,6},{8,9},{9,8},{10,11... | collective-permute-start | bytes 2752520 | tf_op jit(solution)/shard_map/ppermute | solution.py:30
  59.1 7.4 %collective-permute-start.1 = (bf16[896,512]{1,0:T(8,128)(2,1)S(1)}, bf16[896,512]{1,0:T(8,128)(2,1)}, u32[]{:S(2)}, u32[]{:S(2)}) collective-permute-start(bf16[896,512]{1,0:T(8,128)(2,1)S(1)} %bitcast.71), channel_id=1, source_target_pairs={{0,1},{1,0},{2,3},{3,2},{4,5},{5,4},{6,7},{7,6},{8,9},{9,8},{10,11... | collective-permute-start | bytes 2752520 | tf_op jit(solution)/shard_map/ppermute | solution.py:30
  66.5 23.0 %copy-start.3 = (bf16[896,512]{1,0:T(8,128)(2,1)}, bf16[896,512]{1,0:T(8,128)(2,1)S(1)}, u32[]{:S(2)}) copy-start(bf16[896,512]{1,0:T(8,128)(2,1)S(1)} %collective-permute-done.refs_2_) | copy-start | bytes 2752516
  95.0 1.1 copy-start.4
  95.1 94.6 %reduce-scatter.5.cloned.1.call-start = ((), (), s32[]{:S(2)}) async-start(), calls=%async_computation.8 | async-start | bytes 1880064 | tf_op jit(solution)/shard_map/reduce_scatter | solution.py:142
  146.8 30.3 %copy-start.5 = (bf16[1024,896]{1,0:T(8,128)(2,1)S(1)}, bf16[1024,896]{1,0:T(8,128)(2,1)}, u32[]{:S(2)}) copy-start(bf16[1024,896]{1,0:T(8,128)(2,1)} %pad_maximum_fusion) | copy-start | bytes 5505028
  177.2 6.7 %copy-start.6 = (bf16[512,128]{1,0:T(8,128)(2,1)S(1)}, bf16[512,128]{1,0:T(8,128)(2,1)}, u32[]{:S(2)}) copy-start(bf16[512,128]{1,0:T(8,128)(2,1)} %param.14) | copy-start | bytes 393220
  177.2 6.8 %copy-start.8 = (bf16[64,128]{1,0:T(8,128)(2,1)S(1)}, bf16[64,128]{1,0:T(8,128)(2,1)}, u32[]{:S(2)}) copy-start(bf16[64,128]{1,0:T(8,128)(2,1)} %param.15) | copy-start | bytes 49156
  179.0 40.4 %all-to-all-start.1 = ((bf16[16,24,896]{2,1,0:T(8,128)(2,1)}), bf16[16,24,896]{2,1,0:T(8,128)(2,1)S(1)}, u32[]{:S(2)}, u32[]{:S(2)}) async-start(bf16[16,24,896]{2,1,0:T(8,128)(2,1)} %bitcast.76), calls=%async_computation.2 | async-start | bytes 1376256 | tf_op jit(solution)/shard_map/all_to_all | solution.py:72
  183.9 55.3 %all-gather.2.cloned.1.call-start = ((), (), s32[]{:S(2)}) async-start(), calls=%async_computation.6 | async-start | bytes 1327104 | tf_op jit(solution)/shard_map/all_gather | solution.py:20
  217.5 14.1 %copy-start.7 = (bf16[128,256]{1,0:T(8,128)(2,1)S(1)}, bf16[128,256]{1,0:T(8,128)(2,1)}, u32[]{:S(2)}) copy-start(bf16[128,256]{1,0:T(8,128)(2,1)} %param.13) | copy-start | bytes 196612
  219.4 13.9 %copy-start.11 = (f32[256,2]{0,1:T(2,128)S(1)}, f32[256,2]{0,1:T(2,128)}, u32[]{:S(2)}) copy-start(f32[256,2]{0,1:T(2,128)} %param.20) | copy-start | bytes 6148
  219.4 39.9 %all-to-all-start.3 = ((bf16[16,24,896]{2,1,0:T(8,128)(2,1)}), bf16[16,24,896]{2,1,0:T(8,128)(2,1)S(1)}, u32[]{:S(2)}, u32[]{:S(2)}) async-start(bf16[16,24,896]{2,1,0:T(8,128)(2,1)} %bitcast.75), calls=%async_computation.5 | async-start | bytes 1376256 | tf_op jit(solution)/shard_map/all_to_all | solution.py:72
  239.2 1.5 copy-start.9
Sparse Core Ops, SparseCore 0:
  95.2 43.2 reduce-scatter.2
  147.0 42.5 reduce-scatter.4
  192.3 46.8 all-gather.1

commit v5 on v4

--- a/solution.py
+++ b/solution.py
@@ -80,19 +80,22 @@
 
 
 def sums_kernel(rows, gain, *refs):
-    count = len(refs) - 6
+    count = len(refs) - 7
     weights, out = refs[:count], refs[count]
-    gained, fetched, sums, fetch_done, store_done = refs[count + 1 :]
+    taken, gained, fetched, sums, fetch_done, store_done = refs[count + 1 :]
     width = fetched.shape[2]
     fetches = [
         pltpu.make_async_copy(weights[i], fetched.at[i], fetch_done.at[i]) for i in range(count)
     ]
+    take = pltpu.make_async_copy(rows, taken, fetch_done.at[count])
+    take.start()
     for fetch in fetches:
         fetch.start()
-    rows_wide = rows[...].astype(jnp.float32)
+    take.wait()
+    rows_wide = taken[...].astype(jnp.float32)
     gained[...] = (rows_wide * gain[...]).astype(jnp.bfloat16)
     row_sq = jnp.sum(rows_wide * rows_wide, axis=1, keepdims=True)
-    sums[:, count * width :] = jnp.broadcast_to(row_sq, (rows.shape[0], lanes)).astype(jnp.bfloat16)
+    sums[:, count * width :] = jnp.broadcast_to(row_sq, (taken.shape[0], lanes)).astype(jnp.bfloat16)
     ends = [(i + 1) * width for i in range(count - 1)] + [sums.shape[1]]
     stores = []
     for i in range(count):
@@ -117,16 +120,17 @@
         sums_kernel,
         out_shape=jax.ShapeDtypeStruct((row_count, columns), jnp.bfloat16),
         in_specs=[
-            pl.BlockSpec(memory_space=pltpu.VMEM),
+            pl.BlockSpec(memory_space=pl.ANY),
             pl.BlockSpec(memory_space=pltpu.VMEM),
             *[pl.BlockSpec(memory_space=pl.ANY) for _ in weights],
         ],
         out_specs=pl.BlockSpec(memory_space=pl.ANY),
         scratch_shapes=[
             pltpu.VMEM((row_count, width), jnp.bfloat16),
+            pltpu.VMEM((row_count, width), jnp.bfloat16),
             pltpu.VMEM((count, width, block), jnp.bfloat16),
             pltpu.VMEM((row_count, columns), jnp.bfloat16),
-            pltpu.SemaphoreType.DMA((count,)),
+            pltpu.SemaphoreType.DMA((count + 1,)),
             pltpu.SemaphoreType.DMA((count,)),
         ],
         cost_estimate=pl.CostEstimate(
@@ -170,7 +174,6 @@
     w_up,
     w_down,
 ):
-    lat_piece, rope_piece = in_one_piece((latent_keys, rope_keys), "ctx", 1, 0)
     model_width = moe_tokens.shape[1] * lax.axis_size("ctx")
     half_width = w_gate.shape[2]
 
@@ -212,11 +215,11 @@
     in_w = (w_gate[0], w_up[0], of_other_core(w_gate[0], "ep"), of_other_core(w_up[0], "ep"))
     down_w = jnp.concatenate([w_down[0], of_other_core(w_down[0], "ep")], axis=0)
     rows_a, send_b, in_w, down_w = lax.optimization_barrier((rows_a, send_b, in_w, down_w))
-    part_a = activation_sums(rows_a, norm_gain, in_w)
-    part_a, send_b = lax.optimization_barrier((part_a, send_b))
-    share_a = row_shares(part_a)
     rows_b = to_same_core(send_b, expert_count)
+    share_a = row_shares(activation_sums(rows_a, norm_gain, in_w))
     share_b = row_shares(activation_sums(rows_b, norm_gain, in_w))
+    share_b, latent_keys, rope_keys = lax.optimization_barrier((share_b, latent_keys, rope_keys))
+    lat_piece, rope_piece = in_one_piece((latent_keys, rope_keys), "ctx", 1, 0)
     attn_out = attention(q_latent, q_rope, lat_piece, rope_piece, w_uv)
     hidden_a = activations(share_a, model_width, half_width)
     out_a = jnp.dot(hidden_a, down_w, preferred_element_type=jnp.float32).astype(jnp.bfloat16)

time: 269 us -> 271 us (level)
    all_gather x1, waiting for transfers between devices: 5.84 us -> 1.86 us  [in_one_piece(): lax.all_gather(both, axis, axis=dim, tiled=True)]
  transfers between devices with their start and end apart: 9 -> 9, of which waited for: 4 -> 4; matrix products, arithmetic and copies ran while one was open for 7% -> 8% of each run, Pallas kernels for 2% -> 2%
where the time goes in v5:
time: 271 us; the launch traced here: 270 us
  blocking collectives  100 us (37%)
  starting transfers between devices  67.8 us (25%)
  waiting for transfers between devices  48.2 us (18%)
  matrix products  15.6 us (6%)
  between operations  14.2 us (5%)
  Pallas kernels  10.6 us (4%)
  other arithmetic  7.63 us (3%)
  local copies, waits for them, and re-layouts  5.69 us (2%)
    all_to_all x3, starting transfers between devices, to_same_core(): lax.all_to_all(rows.reshape(count, -1, rows.shape[1]), 'ep', split_axis=0...  61.3 us
    all_gather x2, blocking collectives, activations(): return lax.all_gather(part_hidden, 'ctx', axis=0, tiled=True)  55 us
    all_to_all x1, blocking collectives, to_same_core(): lax.all_to_all(rows.reshape(count, -1, rows.shape[1]), 'ep', split_axis=0...  45.2 us
    all_to_all x3, waiting for transfers between devices, to_same_core(): lax.all_to_all(rows.reshape(count, -1, rows.shape[1]), 'ep', split_axis=0...  40 us
    pallas_call x2, Pallas kernels, activation_sums(): pl.pallas_call(sums_kernel, out_shape=jax.ShapeDtypeStruct((row_count, co...  10.6 us
    ppermute x3, starting transfers between devices, of_other_core(): return lax.ppermute(value, axis, [(i, i ^ 1) for i in range(count)])  6.34 us
    reduce_scatter x2, waiting for transfers between devices, row_shares(): return lax.psum_scatter(in_part, 'ctx', scatter_dimension=0, tiled=True)  6.08 us
  transfers between devices with their start and end apart: 9, of which 4 were waited for; matrix products, arithmetic and copies ran while one was open for 8% of the time, Pallas kernels for 2%

profile of v5, /device:TPU:68, one launch (start us, length us, event | category | flops | bytes accessed | tf_op | source)
XLA Modules:
  0.0 269.9 jit_solution(1463800481983794559)
XLA Ops:
  8.6 2.3 convolution_convert_fusion.3
  10.9 43.7 %all-to-all-start = ((bf16[16,24,896]{2,1,0:T(8,128)(2,1)}), bf16[16,24,896]{2,1,0:T(8,128)(2,1)}, u32[]{:S(2)}, u32[]{:S(2)}) async-start(bf16[16,24,896]{2,1,0:T(8,128)(2,1)} %bitcast.4), calls=%async_computation | async-start | bytes 1376256 | tf_op jit(solution)/shard_map/all_to_all | solution.py:72
  54.7 2.0 collective-permute-start.2
  56.6 2.4 collective-permute-start
  59.1 2.0 collective-permute-start.1
  61.7 2.3 convolution_convert_fusion.2
  63.9 2.6 pad_maximum_fusion
  66.5 23.0 %all-to-all-done = bf16[16,24,896]{2,1,0:T(8,128)(2,1)} async-done(((bf16[16,24,896]{2,1,0:T(8,128)(2,1)}), bf16[16,24,896]{2,1,0:T(8,128)(2,1)}, u32[]{:S(2)}, u32[]{:S(2)}) %all-to-all-start) | async-done | bytes 688160 | tf_op jit(solution)/shard_map/all_to_all | solution.py:72
  89.5 5.3 %gate_up_sums.3 = bf16[384,2176]{1,0:T(8,128)(2,1)} custom-call(bf16[384,896]{1,0:T(8,128)(2,1)} %bitcast.5.rows, f32[1,896]{1,0:T(1,128)} %broadcast_in_dim.69.gain, bf16[896,512]{1,0:T(8,128)(2,1)} %bitcast.66, bf16[896,512]{1,0:T(8,128)(2,1)} %bitcast.69, bf16[896,512]{1,0:T(8,128)(2,1)} %copy-done.3, bf16[896,512]{1,0:T(8,128)(2,1)} %collective-permute-done.1.refs_3_), custom_call_target="tpu_custom_call" | custom-call | flops 1409286144 | bytes 6029312 | tf_op jit(solution)/shard_map/gate_up_sums/pallas_call | solution.py:119
  95.9 45.2 %all_to_all.20 = bf16[16,24,896]{2,1,0:T(8,128)(2,1)} all-to-all(bf16[16,24,896]{2,1,0:T(8,128)(2,1)S(1)} %bitcast.73), channel_id=1, replica_groups={{0,2,4,6,8,10,12,14,16,18,20,22,24,26,28,30},{1,3,5,7,9,11,13,15,17,19,..., dimensions={0} | all-to-all | bytes 1376256 | tf_op jit(solution)/shard_map/all_to_all | solution.py:72
  141.2 5.3 %gate_up_sums.2 = bf16[384,2176]{1,0:T(8,128)(2,1)} custom-call(bf16[384,896]{1,0:T(8,128)(2,1)} %bitcast.72, f32[1,896]{1,0:T(1,128)} %broadcast_in_dim.69.gain, bf16[896,512]{1,0:T(8,128)(2,1)} %bitcast.67, bf16[896,512]{1,0:T(8,128)(2,1)} %bitcast.70, bf16[896,512]{1,0:T(8,128)(2,1)} %copy-done.3, bf16[896,512]{1,0:T(8,128)(2,1)} %collective-permute-done.1.refs_3_), custom_call_target="tpu_custom_call" | custom-call | flops 1409286144 | bytes 6029312 | tf_op jit(solution)/shard_map/gate_up_sums/pallas_call | solution.py:119
  148.0 28.8 %all_gather.10 = bf16[384,1024]{1,0:T(8,128)(2,1)S(1)} all-gather(bf16[48,1024]{1,0:T(8,128)(2,1)S(1)} %pad_maximum_fusion.2), channel_id=1, replica_groups=mesh['group'=2,'ctx'=8,'ep'=32] {'ctx'}, dimensions={0}, use_global_device_ids=true | all-gather | bytes 884736 | tf_op jit(solution)/shard_map/all_gather | solution.py:160
  176.8 1.8 convolution_convert_fusion.1
  178.6 4.8 %all-to-all-start.2 = ((bf16[16,24,896]{2,1,0:T(8,128)(2,1)}), bf16[16,24,896]{2,1,0:T(8,128)(2,1)S(1)}, u32[]{:S(2)}, u32[]{:S(2)}) async-start(bf16[16,24,896]{2,1,0:T(8,128)(2,1)} %bitcast.76), calls=%async_computation.4 | async-start | bytes 1376256 | tf_op jit(solution)/shard_map/all_to_all | solution.py:72
  183.4 6.1 %reduce-scatter.3.cloned.1.call-done = bf16[48,2176]{1,0:T(8,128)(2,1)} async-done(((bf16[384,2176]{1,0:T(8,128)(2,1)}), bf16[48,2176]{1,0:T(8,128)(2,1)}) %reduce-scatter.3.cloned.1.call-update) | async-done | bytes 208912 | tf_op jit(solution)/shard_map/reduce_scatter | solution.py:146
  190.5 1.6 pad_maximum_fusion.1
  192.5 26.3 %all_gather.11 = bf16[384,1024]{1,0:T(8,128)(2,1)S(1)} all-gather(bf16[48,1024]{1,0:T(8,128)(2,1)S(1)} %pad_maximum_fusion.3), channel_id=1, replica_groups=mesh['group'=2,'ctx'=8,'ep'=32] {'ctx'}, dimensions={0}, use_global_device_ids=true | all-gather | bytes 884736 | tf_op jit(solution)/shard_map/all_gather | solution.py:160
  218.8 1.8 convolution_convert_fusion
  220.6 12.8 %all-to-all-start.3 = ((bf16[16,24,896]{2,1,0:T(8,128)(2,1)}), bf16[16,24,896]{2,1,0:T(8,128)(2,1)S(1)}, u32[]{:S(2)}, u32[]{:S(2)}) async-start(bf16[16,24,896]{2,1,0:T(8,128)(2,1)} %bitcast.75), calls=%async_computation.5 | async-start | bytes 1376256 | tf_op jit(solution)/shard_map/all_to_all | solution.py:72
  233.6 1.3 copy.20
  235.2 1.4 convolution_bitcast_fusion.2
  236.6 1.9 all-gather.2.cloned.1.call-done
  238.5 1.5 fusion.33
  243.3 17.0 %all-to-all-done.3 = bf16[16,24,896]{2,1,0:T(8,128)(2,1)S(1)} async-done(((bf16[16,24,896]{2,1,0:T(8,128)(2,1)}), bf16[16,24,896]{2,1,0:T(8,128)(2,1)S(1)}, u32[]{:S(2)}, u32[]{:S(2)}) %all-to-all-start.3) | async-done | bytes 688160 | tf_op jit(solution)/shard_map/all_to_all | solution.py:72
  (68 shorter events, 12.8 us)
Async XLA Ops:
  7.2 235.0 %copy-start = (bf16[4,512,128]{2,1,0:T(8,128)(2,1)S(1)}, bf16[4,512,128]{2,1,0:T(8,128)(2,1)}, u32[]{:S(2)}) copy-start(bf16[4,512,128]{2,1,0:T(8,128)(2,1)} %param.16) | copy-start | bytes 1572868
  7.2 49.4 %copy-start.1 = (bf16[1,896,512]{2,1,0:T(8,128)(2,1)S(1)}, bf16[1,896,512]{2,1,0:T(8,128)(2,1)}, u32[]{:S(2)}) copy-start(bf16[1,896,512]{2,1,0:T(8,128)(2,1)} %param.21) | copy-start | bytes 2752516
  7.2 51.9 %copy-start.2 = (bf16[1,896,512]{2,1,0:T(8,128)(2,1)S(1)}, bf16[1,896,512]{2,1,0:T(8,128)(2,1)}, u32[]{:S(2)}) copy-start(bf16[1,896,512]{2,1,0:T(8,128)(2,1)} %param.22) | copy-start | bytes 2752516
  7.2 53.8 %copy-start.9 = (f32[896]{0:T(1024)S(1)}, f32[896]{0:T(1024)}, u32[]{:S(2)}) copy-start(f32[896]{0:T(1024)} %param.18) | copy-start | bytes 10756
  10.9 78.6 %all-to-all-start = ((bf16[16,24,896]{2,1,0:T(8,128)(2,1)}), bf16[16,24,896]{2,1,0:T(8,128)(2,1)}, u32[]{:S(2)}, u32[]{:S(2)}) async-start(bf16[16,24,896]{2,1,0:T(8,128)(2,1)} %bitcast.4), calls=%async_computation | async-start | bytes 1376256 | tf_op jit(solution)/shard_map/all_to_all | solution.py:72
  54.6 91.9 %reduce-scatter.5.cloned.1.call-start = ((), (), s32[]{:S(2)}) async-start(), calls=%async_computation.8 | async-start | bytes 1880064 | tf_op jit(solution)/shard_map/reduce_scatter | solution.py:146
  54.7 9.2 %collective-permute-start.2 = (bf16[512,896]{1,0:T(8,128)(2,1)}, bf16[512,896]{1,0:T(8,128)(2,1)S(1)}, u32[]{:S(2)}, u32[]{:S(2)}) collective-permute-start(bf16[512,896]{1,0:T(8,128)(2,1)} %bitcast.8), channel_id=1, source_target_pairs={{0,1},{1,0},{2,3},{3,2},{4,5},{5,4},{6,7},{7,6},{8,9},{9,8},{10,11... | collective-permute-start | bytes 2752520 | tf_op jit(solution)/shard_map/ppermute | solution.py:30
  56.6 9.9 %collective-permute-start = (bf16[896,512]{1,0:T(8,128)(2,1)S(1)}, bf16[896,512]{1,0:T(8,128)(2,1)S(1)}, u32[]{:S(2)}, u32[]{:S(2)}) collective-permute-start(bf16[896,512]{1,0:T(8,128)(2,1)S(1)} %bitcast.68), channel_id=1, source_target_pairs={{0,1},{1,0},{2,3},{3,2},{4,5},{5,4},{6,7},{7,6},{8,9},{9,8},{10,11... | collective-permute-start | bytes 2752520 | tf_op jit(solution)/shard_map/ppermute | solution.py:30
  59.1 7.4 %collective-permute-start.1 = (bf16[896,512]{1,0:T(8,128)(2,1)S(1)}, bf16[896,512]{1,0:T(8,128)(2,1)}, u32[]{:S(2)}, u32[]{:S(2)}) collective-permute-start(bf16[896,512]{1,0:T(8,128)(2,1)S(1)} %bitcast.71), channel_id=1, source_target_pairs={{0,1},{1,0},{2,3},{3,2},{4,5},{5,4},{6,7},{7,6},{8,9},{9,8},{10,11... | collective-permute-start | bytes 2752520 | tf_op jit(solution)/shard_map/ppermute | solution.py:30
  66.5 23.0 %copy-start.3 = (bf16[896,512]{1,0:T(8,128)(2,1)}, bf16[896,512]{1,0:T(8,128)(2,1)S(1)}, u32[]{:S(2)}) copy-start(bf16[896,512]{1,0:T(8,128)(2,1)S(1)} %collective-permute-done.refs_2_) | copy-start | bytes 2752516
  94.8 1.1 copy-start.4
  94.9 94.6 %reduce-scatter.3.cloned.1.call-start = ((), (), s32[]{:S(2)}) async-start(), calls=%async_computation.6 | async-start | bytes 1880064 | tf_op jit(solution)/shard_map/reduce_scatter | solution.py:146
  146.4 30.3 %copy-start.5 = (bf16[1024,896]{1,0:T(8,128)(2,1)S(1)}, bf16[1024,896]{1,0:T(8,128)(2,1)}, u32[]{:S(2)}) copy-start(bf16[1024,896]{1,0:T(8,128)(2,1)} %pad_maximum_fusion) | copy-start | bytes 5505028
  176.8 13.7 %copy-start.7 = (bf16[64,128]{1,0:T(8,128)(2,1)S(1)}, bf16[64,128]{1,0:T(8,128)(2,1)}, u32[]{:S(2)}) copy-start(bf16[64,128]{1,0:T(8,128)(2,1)} %param.15) | copy-start | bytes 49156
  178.6 42.0 %all-to-all-start.2 = ((bf16[16,24,896]{2,1,0:T(8,128)(2,1)}), bf16[16,24,896]{2,1,0:T(8,128)(2,1)S(1)}, u32[]{:S(2)}, u32[]{:S(2)}) async-start(bf16[16,24,896]{2,1,0:T(8,128)(2,1)} %bitcast.76), calls=%async_computation.4 | async-start | bytes 1376256 | tf_op jit(solution)/shard_map/all_to_all | solution.py:72
  183.4 55.1 %all-gather.2.cloned.1.call-start = ((), (), s32[]{:S(2)}) async-start(), calls=%async_computation.7 | async-start | bytes 1327104 | tf_op jit(solution)/shard_map/all_gather | solution.py:20
  218.8 14.7 %copy-start.6 = (bf16[128,256]{1,0:T(8,128)(2,1)S(1)}, bf16[128,256]{1,0:T(8,128)(2,1)}, u32[]{:S(2)}) copy-start(bf16[128,256]{1,0:T(8,128)(2,1)} %param.13) | copy-start | bytes 196612
  220.6 14.5 %copy-start.10 = (f32[256,2]{0,1:T(2,128)S(1)}, f32[256,2]{0,1:T(2,128)}, u32[]{:S(2)}) copy-start(f32[256,2]{0,1:T(2,128)} %param.20) | copy-start | bytes 6148
  220.6 39.8 %all-to-all-start.3 = ((bf16[16,24,896]{2,1,0:T(8,128)(2,1)}), bf16[16,24,896]{2,1,0:T(8,128)(2,1)S(1)}, u32[]{:S(2)}, u32[]{:S(2)}) async-start(bf16[16,24,896]{2,1,0:T(8,128)(2,1)} %bitcast.75), calls=%async_computation.5 | async-start | bytes 1376256 | tf_op jit(solution)/shard_map/all_to_all | solution.py:72
  238.5 1.5 copy-start.8
  260.9 1.2 copy-start.11
Sparse Core Ops, SparseCore 0:
  95.0 43.1 reduce-scatter.4
  146.6 42.8 reduce-scatter.2
  192.2 46.1 all-gather.1

commit v6 on v3

--- a/solution.py
+++ b/solution.py
@@ -7,15 +7,6 @@
 norm_eps = 1e-06
 neg_large = -1e30
 lanes = 128
-
-
-def in_one_piece(arrays, axis, dim, along):
-    ends, at = ([], 0)
-    for a in arrays[:-1]:
-        at += a.shape[along]
-        ends.append(at)
-    both = jnp.concatenate(arrays, axis=along)
-    return tuple(jnp.split(lax.all_gather(both, axis, axis=dim, tiled=True), ends, axis=along))
 
 
 def same_core(axis):
@@ -90,17 +81,12 @@
     return lax.psum_scatter(in_part, "ctx", scatter_dimension=0, tiled=True)
 
 
-def activations(row_share, model_width, half_width):
-    row_share = row_share.astype(jnp.float32)
-    row_scale = lax.rsqrt(row_share[:, -1:] / model_width + norm_eps)
-    sums = row_share[:, :-lanes] * row_scale
-    part_hidden = jnp.concatenate(
-        [
-            jax.nn.silu(sums[:, at : at + half_width]) * sums[:, at + half_width : at + 2 * half_width]
-            for at in (0, 2 * half_width)
-        ],
-        axis=1,
-    ).astype(jnp.bfloat16)
+def activations(row_share, model_width):
+    width = (row_share.shape[1] - lanes) // 2
+    row_scale = lax.rsqrt(row_share[:, -1:].astype(jnp.float32) / model_width + norm_eps)
+    gate = row_share[:, :width].astype(jnp.float32) * row_scale
+    up = row_share[:, width : 2 * width].astype(jnp.float32) * row_scale
+    part_hidden = (jax.nn.silu(gate) * up).astype(jnp.bfloat16)
     return lax.all_gather(part_hidden, "ctx", axis=0, tiled=True)
 
 
@@ -119,7 +105,6 @@
     w_down,
 ):
     model_width = moe_tokens.shape[1] * lax.axis_size("ctx")
-    half_width = w_gate.shape[2]
 
     tok_rows, top_count = expert_ids.shape
     expert_count = lax.axis_size("ep") // 2
@@ -136,53 +121,56 @@
     slot = jnp.dot(member.astype(jnp.bfloat16), earlier, preferred_element_type=jnp.float32)
     slot = jnp.where(member > 0.0, slot, -1.0)
 
-    def placed(at):
+    def placed(slots, at):
         wanted = jnp.arange(at * chunk, (at + 1) * chunk, dtype=jnp.int32).astype(jnp.float32)
-        return slot[:, None, :] == wanted[None, :, None]
+        return slots[:, None, :] == wanted[None, :, None]
 
-    def sent_rows(at):
-        route_map = placed(at).astype(jnp.bfloat16).reshape(expert_count * chunk, tok_rows)
+    def sent_rows(slots, at):
+        route_map = jnp.where(placed(slots, at), 1.0, 0.0).astype(jnp.bfloat16)
+        route_map = route_map.reshape(expert_count * chunk, tok_rows)
         return jnp.dot(route_map, moe_tokens, preferred_element_type=jnp.float32).astype(jnp.bfloat16)
 
-    def weighted_sum(at, back):
-        weights = jnp.where(placed(at), expert_weight[:, None, :], 0.0)
-        weights = weights.reshape(expert_count * chunk, tok_rows)
-        high = weights.astype(jnp.bfloat16)
-        low = (weights - high.astype(jnp.float32)).astype(jnp.bfloat16)
-        return sum(
-            lax.dot_general(part, back, (((0,), (0,)), ((), ())), preferred_element_type=jnp.float32)
-            for part in (high, low)
-        )
+    def return_weights(slots, at):
+        weights = jnp.where(placed(slots, at), expert_weight[:, None, :], 0.0).astype(jnp.bfloat16)
+        return weights.reshape(expert_count * chunk, tok_rows).T
 
-    rows_a = to_same_core(sent_rows(0), expert_count)
-    send_b = sent_rows(1)
+    rows_a = to_same_core(sent_rows(slot, 0), expert_count)
+    slot_b, slot_back = lax.optimization_barrier((slot, slot))
+    send_b = sent_rows(slot_b, 1)
     in_w = jnp.concatenate(
         [
             w_gate[0],
+            of_other_core(w_gate[0], "ep"),
             w_up[0],
-            of_other_core(w_gate[0], "ep"),
             of_other_core(w_up[0], "ep"),
             jnp.zeros((w_gate.shape[1], lanes), jnp.bfloat16),
         ],
         axis=1,
     )
     down_w = jnp.concatenate([w_down[0], of_other_core(w_down[0], "ep")], axis=0)
-    rows_a, send_b, in_w, down_w = lax.optimization_barrier((rows_a, send_b, in_w, down_w))
+    weights_a, weights_b = (return_weights(slot_back, at) for at in range(2))
+    own_keys = jnp.concatenate([latent_keys, rope_keys], axis=0)
+    rows_a, send_b, in_w, down_w, weights_a, weights_b, own_keys = lax.optimization_barrier(
+        (rows_a, send_b, in_w, down_w, weights_a, weights_b, own_keys)
+    )
     part_a = activation_sums(rows_a, norm_gain, in_w)
     part_a, send_b = lax.optimization_barrier((part_a, send_b))
     share_a = row_shares(part_a)
     rows_b = to_same_core(send_b, expert_count)
     share_b = row_shares(activation_sums(rows_b, norm_gain, in_w))
-    share_b, latent_keys, rope_keys = lax.optimization_barrier((share_b, latent_keys, rope_keys))
-    lat_piece, rope_piece = in_one_piece((latent_keys, rope_keys), "ctx", 1, 0)
+    share_b, own_keys = lax.optimization_barrier((share_b, own_keys))
+    all_keys = lax.all_gather(own_keys, "ctx", axis=1, tiled=True)
+    lat_piece, rope_piece = jnp.split(all_keys, [latent_keys.shape[0]], axis=0)
     attn_out = attention(q_latent, q_rope, lat_piece, rope_piece, w_uv)
-    hidden_a = activations(share_a, model_width, half_width)
+    hidden_a = activations(share_a, model_width)
     out_a = jnp.dot(hidden_a, down_w, preferred_element_type=jnp.float32).astype(jnp.bfloat16)
     back_a = to_same_core(out_a, expert_count)
-    hidden_b = activations(share_b, model_width, half_width)
+    hidden_b = activations(share_b, model_width)
     out_b = jnp.dot(hidden_b, down_w, preferred_element_type=jnp.float32).astype(jnp.bfloat16)
     back_b = to_same_core(out_b, expert_count)
-    moe_out = (weighted_sum(0, back_a) + weighted_sum(1, back_b)).astype(jnp.bfloat16)
+    mixed = jnp.dot(weights_a, back_a, preferred_element_type=jnp.float32)
+    moe_out = mixed + jnp.dot(weights_b, back_b, preferred_element_type=jnp.float32)
+    moe_out = moe_out.astype(jnp.bfloat16)
     return (attn_out, moe_out)
 
 

time: 285 us -> 316 us (1.11)
  the two profiles are of different devices: /device:TPU:66 before, /device:TPU:68 now
where the time goes in v6:
time: 316 us; the launch traced here: 315 us
  blocking collectives  98.7 us (31%)
  waiting for transfers between devices  80.7 us (26%)
  starting transfers between devices  76.6 us (24%)
  matrix products  22.3 us (7%)
  between operations  14.1 us (4%)
  local copies, waits for them, and re-layouts  13.2 us (4%)
  other arithmetic  9.38 us (3%)
    all_to_all x3, starting transfers between devices, to_same_core(): lax.all_to_all(rows.reshape(count, -1, rows.shape[1]), 'ep', split_axis=0...  70 us
    all_gather x2, blocking collectives, activations(): return lax.all_gather(part_hidden, 'ctx', axis=0, tiled=True)  53.6 us
    reduce_scatter x2, waiting for transfers between devices, row_shares(): return lax.psum_scatter(in_part, 'ctx', scatter_dimension=0, tiled=True)  45.4 us
    all_to_all x1, blocking collectives, to_same_core(): lax.all_to_all(rows.reshape(count, -1, rows.shape[1]), 'ep', split_axis=0...  45.1 us
    all_to_all x3, waiting for transfers between devices, to_same_core(): lax.all_to_all(rows.reshape(count, -1, rows.shape[1]), 'ep', split_axis=0...  30.4 us
    unnamed x29, local copies, waits for them, and re-layouts  11.2 us
    dot_general x2, matrix products, activation_sums(): in_part = jnp.dot(gained, in_w, preferred_element_type=jnp.float32)  10.7 us
    ppermute x3, starting transfers between devices, of_other_core(): return lax.ppermute(value, axis, [(i, i ^ 1) for i in range(count)])  6.35 us
  transfers between devices with their start and end apart: 9, of which 5 were waited for; matrix products, arithmetic and copies ran while one was open for 9% of the time, Pallas kernels for 0%

profile of v6, /device:TPU:68, one launch (start us, length us, event | category | flops | bytes accessed | tf_op | source)
XLA Modules:
  0.0 314.9 jit_solution(16299748828319527868)
XLA Ops:
  8.4 2.3 convolution_convert_fusion.3
  10.7 43.8 %all-to-all-start = ((bf16[16,24,896]{2,1,0:T(8,128)(2,1)}), bf16[16,24,896]{2,1,0:T(8,128)(2,1)S(1)}, u32[]{:S(2)}, u32[]{:S(2)}) async-start(bf16[16,24,896]{2,1,0:T(8,128)(2,1)} %bitcast.4), calls=%async_computation | async-start | bytes 1376256 | tf_op jit(solution)/shard_map/all_to_all | solution.py:61
  54.6 2.0 collective-permute-start
  56.6 2.4 collective-permute-start.1
  59.0 2.0 collective-permute-start.2
  61.0 2.2 constant_dynamic-update-slice_fusion.3
  65.4 2.2 constant_dynamic-update-slice_fusion.2
  67.6 2.2 constant_dynamic-update-slice_fusion.1
  69.8 2.3 constant_dynamic-update-slice_fusion
  72.8 2.6 pad_maximum_fusion
  75.4 14.0 %all-to-all-done = bf16[16,24,896]{2,1,0:T(8,128)(2,1)S(1)} async-done(((bf16[16,24,896]{2,1,0:T(8,128)(2,1)}), bf16[16,24,896]{2,1,0:T(8,128)(2,1)S(1)}, u32[]{:S(2)}, u32[]{:S(2)}) %all-to-all-start) | async-done | bytes 688160 | tf_op jit(solution)/shard_map/all_to_all | solution.py:61
  89.6 5.3 %fusion = bf16[384,2176]{1,0:T(8,128)(2,1)} fusion(bf16[896,2176]{1,0:T(8,128)(2,1)} %broadcast_dynamic-update-slice_fusion, bf16[384]{0:T(512)(128)(2,1)S(1)} %fusion.5, pred[2176]{0:T(1024)(128)(4,1)S(1)} %iota_compare_fusion.5, bf16[384,896]{1,0:T(8,128)(2,1)S(1)} %bitcast.83, f32[896]{0:T(1024)S(1)} %copy-done.9), kind=kOutput, calls=%fused_computation.2 | convolution fusion | flops 1499234304 | bytes 6265216 | tf_op jit(solution)/shard_map/dot_general | solution.py:75
  94.8 45.1 %all_to_all.20 = bf16[16,24,896]{2,1,0:T(8,128)(2,1)S(1)} all-to-all(bf16[16,24,896]{2,1,0:T(8,128)(2,1)S(1)} %bitcast.85), channel_id=1, replica_groups={{0,2,4,6,8,10,12,14,16,18,20,22,24,26,28,30},{1,3,5,7,9,11,13,15,17,19,..., dimensions={0} | all-to-all | bytes 1376256 | tf_op jit(solution)/shard_map/all_to_all | solution.py:61
  140.4 5.4 %fusion.1 = bf16[384,2176]{1,0:T(8,128)(2,1)} fusion(bf16[384,896]{1,0:T(8,128)(2,1)S(1)} %fusion.6, bf16[896,2176]{1,0:T(8,128)(2,1)} %broadcast_dynamic-update-slice_fusion, bf16[384]{0:T(512)(128)(2,1)S(1)} %broadcast_in_dim.107, pred[2176]{0:T(1024)(128)(4,1)S(1)} %iota_compare_fusion.5), kind=kOutput, calls=%fused_computation.3 | convolution fusion | flops 1498202112 | bytes 6261632 | tf_op jit(solution)/shard_map/dot_general | solution.py:75
  146.7 40.1 %reduce-scatter.3.cloned.1.call-done = bf16[48,2176]{1,0:T(8,128)(2,1)} async-done(((bf16[384,2176]{1,0:T(8,128)(2,1)}), bf16[48,2176]{1,0:T(8,128)(2,1)}) %reduce-scatter.3.cloned.1.call-update) | async-done | bytes 208912 | tf_op jit(solution)/shard_map/reduce_scatter | solution.py:81
  188.7 26.9 %all_gather.11 = bf16[384,1024]{1,0:T(8,128)(2,1)S(1)} all-gather(bf16[48,1024]{1,0:T(8,128)(2,1)S(1)} %multiply_convert_fusion), channel_id=1, replica_groups=mesh['group'=2,'ctx'=8,'ep'=32] {'ctx'}, dimensions={0}, use_global_device_ids=true | all-gather | bytes 884736 | tf_op jit(solution)/shard_map/all_gather | solution.py:90
  215.6 1.9 convolution_convert_fusion
  217.5 13.1 %all-to-all-start.3 = ((bf16[16,24,896]{2,1,0:T(8,128)(2,1)}), bf16[16,24,896]{2,1,0:T(8,128)(2,1)S(1)}, u32[]{:S(2)}, u32[]{:S(2)}) async-start(bf16[16,24,896]{2,1,0:T(8,128)(2,1)} %bitcast.92), calls=%async_computation.5 | async-start | bytes 1376256 | tf_op jit(solution)/shard_map/all_to_all | solution.py:61
  231.5 5.4 %reduce-scatter.5.cloned.1.call-done = bf16[48,2176]{1,0:T(8,128)(2,1)} async-done(((bf16[384,2176]{1,0:T(8,128)(2,1)}), bf16[48,2176]{1,0:T(8,128)(2,1)}) %reduce-scatter.5.cloned.1.call-update) | async-done | bytes 208912 | tf_op jit(solution)/shard_map/reduce_scatter | solution.py:81
  238.8 26.6 %all_gather.10 = bf16[384,1024]{1,0:T(8,128)(2,1)S(1)} all-gather(bf16[48,1024]{1,0:T(8,128)(2,1)S(1)} %multiply_convert_fusion.1), channel_id=1, replica_groups=mesh['group'=2,'ctx'=8,'ep'=32] {'ctx'}, dimensions={0}, use_global_device_ids=true | all-gather | bytes 884736 | tf_op jit(solution)/shard_map/all_gather | solution.py:90
  265.5 1.8 convolution_convert_fusion.1
  267.3 13.1 %all-to-all-start.2 = ((bf16[16,24,896]{2,1,0:T(8,128)(2,1)}), bf16[16,24,896]{2,1,0:T(8,128)(2,1)S(1)}, u32[]{:S(2)}, u32[]{:S(2)}) async-start(bf16[16,24,896]{2,1,0:T(8,128)(2,1)} %bitcast.91), calls=%async_computation.4 | async-start | bytes 1376256 | tf_op jit(solution)/shard_map/all_to_all | solution.py:61
  282.1 3.4 %all-gather.2.cloned.1.call-done = bf16[576,1024]{1,0:T(8,128)(2,1)} async-done(((bf16[576,128]{1,0:T(8,128)(2,1)}), bf16[576,1024]{1,0:T(8,128)(2,1)}) %all-gather.2.cloned.1.call-update) | async-done | bytes 1179664 | tf_op jit(solution)/shard_map/all_gather | solution.py:162
  290.7 16.4 %all-to-all-done.2 = bf16[16,24,896]{2,1,0:T(8,128)(2,1)S(1)} async-done(((bf16[16,24,896]{2,1,0:T(8,128)(2,1)}), bf16[16,24,896]{2,1,0:T(8,128)(2,1)S(1)}, u32[]{:S(2)}, u32[]{:S(2)}) %all-to-all-start.2) | async-done | bytes 688160 | tf_op jit(solution)/shard_map/all_to_all | solution.py:61
  (69 shorter events, 18.5 us)
Async XLA Ops:
  7.2 282.0 %copy-start = (bf16[4,512,128]{2,1,0:T(8,128)(2,1)S(1)}, bf16[4,512,128]{2,1,0:T(8,128)(2,1)}, u32[]{:S(2)}) copy-start(bf16[4,512,128]{2,1,0:T(8,128)(2,1)} %param.16) | copy-start | bytes 1572868
  7.2 51.8 %copy-start.3 = (bf16[1,512,896]{2,1,0:T(8,128)(2,1)S(1)}, bf16[1,512,896]{2,1,0:T(8,128)(2,1)}, u32[]{:S(2)}) copy-start(bf16[1,512,896]{2,1,0:T(8,128)(2,1)} %param.23) | copy-start | bytes 2752516
  7.2 53.8 %copy-start.10 = (f32[256,2]{0,1:T(2,128)S(1)}, f32[256,2]{0,1:T(2,128)}, u32[]{:S(2)}) copy-start(f32[256,2]{0,1:T(2,128)} %param.20) | copy-start | bytes 6148
  8.4 54.8 %copy-start.5 = (bf16[512,128]{1,0:T(8,128)(2,1)S(1)}, bf16[512,128]{1,0:T(8,128)(2,1)}, u32[]{:S(2)}) copy-start(bf16[512,128]{1,0:T(8,128)(2,1)} %param.14) | copy-start | bytes 393220
  8.4 54.8 %copy-start.7 = (bf16[64,128]{1,0:T(8,128)(2,1)S(1)}, bf16[64,128]{1,0:T(8,128)(2,1)}, u32[]{:S(2)}) copy-start(bf16[64,128]{1,0:T(8,128)(2,1)} %param.15) | copy-start | bytes 49156
  10.7 54.3 %copy-start.2 = (bf16[256,896]{1,0:T(8,128)(2,1)S(1)}, bf16[256,896]{1,0:T(8,128)(2,1)}, u32[]{:S(2)}) copy-start(bf16[256,896]{1,0:T(8,128)(2,1)} %param.17) | copy-start | bytes 1376260
  10.7 78.6 %all-to-all-start = ((bf16[16,24,896]{2,1,0:T(8,128)(2,1)}), bf16[16,24,896]{2,1,0:T(8,128)(2,1)S(1)}, u32[]{:S(2)}, u32[]{:S(2)}) async-start(bf16[16,24,896]{2,1,0:T(8,128)(2,1)} %bitcast.4), calls=%async_computation | async-start | bytes 1376256 | tf_op jit(solution)/shard_map/all_to_all | solution.py:61
  54.5 132.2 %reduce-scatter.3.cloned.1.call-start = ((), (), s32[]{:S(2)}) async-start(), calls=%async_computation.6 | async-start | bytes 1880064 | tf_op jit(solution)/shard_map/reduce_scatter | solution.py:81
  54.6 10.8 %collective-permute-start = (bf16[896,512]{1,0:T(8,128)(2,1)}, bf16[896,512]{1,0:T(8,128)(2,1)}, u32[]{:S(2)}, u32[]{:S(2)}) collective-permute-start(bf16[896,512]{1,0:T(8,128)(2,1)} %bitcast.7), channel_id=1, source_target_pairs={{0,1},{1,0},{2,3},{3,2},{4,5},{5,4},{6,7},{7,6},{8,9},{9,8},{10,11... | collective-permute-start | bytes 2752520 | tf_op jit(solution)/shard_map/ppermute | solution.py:19
  56.6 13.2 %collective-permute-start.1 = (bf16[896,512]{1,0:T(8,128)(2,1)}, bf16[896,512]{1,0:T(8,128)(2,1)}, u32[]{:S(2)}, u32[]{:S(2)}) collective-permute-start(bf16[896,512]{1,0:T(8,128)(2,1)} %bitcast.8), channel_id=1, source_target_pairs={{0,1},{1,0},{2,3},{3,2},{4,5},{5,4},{6,7},{7,6},{8,9},{9,8},{10,11... | collective-permute-start | bytes 2752520 | tf_op jit(solution)/shard_map/ppermute | solution.py:19
  59.0 13.8 %collective-permute-start.2 = (bf16[512,896]{1,0:T(8,128)(2,1)S(1)}, bf16[512,896]{1,0:T(8,128)(2,1)}, u32[]{:S(2)}, u32[]{:S(2)}) collective-permute-start(bf16[512,896]{1,0:T(8,128)(2,1)S(1)} %bitcast.87), channel_id=1, source_target_pairs={{0,1},{1,0},{2,3},{3,2},{4,5},{5,4},{6,7},{7,6},{8,9},{9,8},{10,11... | collective-permute-start | bytes 2752520 | tf_op jit(solution)/shard_map/ppermute | solution.py:19
  72.8 16.8 %copy-start.9 = (f32[896]{0:T(1024)S(1)}, f32[896]{0:T(1024)}, u32[]{:S(2)}) copy-start(f32[896]{0:T(1024)} %param.18) | copy-start | bytes 10756
  145.8 69.9 %copy-start.1 = (bf16[1024,896]{1,0:T(8,128)(2,1)S(1)}, bf16[1024,896]{1,0:T(8,128)(2,1)}, u32[]{:S(2)}) copy-start(bf16[1024,896]{1,0:T(8,128)(2,1)} %pad_maximum_fusion) | copy-start | bytes 5505028
  145.8 91.0 %reduce-scatter.5.cloned.1.call-start = ((), (), s32[]{:S(2)}) async-start(), calls=%async_computation.8 | async-start | bytes 1880064 | tf_op jit(solution)/shard_map/reduce_scatter | solution.py:81
  217.5 49.8 %all-to-all-start.3 = ((bf16[16,24,896]{2,1,0:T(8,128)(2,1)}), bf16[16,24,896]{2,1,0:T(8,128)(2,1)S(1)}, u32[]{:S(2)}, u32[]{:S(2)}) async-start(bf16[16,24,896]{2,1,0:T(8,128)(2,1)} %bitcast.92), calls=%async_computation.5 | async-start | bytes 1376256 | tf_op jit(solution)/shard_map/all_to_all | solution.py:61
  230.7 54.8 %all-gather.2.cloned.1.call-start = ((), (), s32[]{:S(2)}) async-start(), calls=%async_computation.7 | async-start | bytes 1327104 | tf_op jit(solution)/shard_map/all_gather | solution.py:162
  265.5 14.9 %copy-start.6 = (bf16[128,256]{1,0:T(8,128)(2,1)S(1)}, bf16[128,256]{1,0:T(8,128)(2,1)}, u32[]{:S(2)}) copy-start(bf16[128,256]{1,0:T(8,128)(2,1)} %param.13) | copy-start | bytes 196612
  267.3 39.8 %all-to-all-start.2 = ((bf16[16,24,896]{2,1,0:T(8,128)(2,1)}), bf16[16,24,896]{2,1,0:T(8,128)(2,1)S(1)}, u32[]{:S(2)}, u32[]{:S(2)}) async-start(bf16[16,24,896]{2,1,0:T(8,128)(2,1)} %bitcast.91), calls=%async_computation.4 | async-start | bytes 1376256 | tf_op jit(solution)/shard_map/all_to_all | solution.py:61
  285.4 1.5 copy-start.8
  288.4 1.9 copy-start.4
Sparse Core Ops, SparseCore 0:
  146.0 40.7 reduce-scatter.2
  189.6 47.2 reduce-scatter.4
  238.9 46.5 all-gather.1

commit v7 on v6

--- a/solution.py
+++ b/solution.py
@@ -9,9 +9,9 @@
 lanes = 128
 
 
-def same_core(axis):
-    count = lax.axis_size(axis)
-    return [list(range(core, count, 2)) for core in range(2)]
+def one_core_each(axis):
+    chips = range(lax.axis_size(axis) // 2)
+    return [[2 * chip + (chip + turn) % 2 for chip in chips] for turn in range(2)]
 
 
 def of_other_core(value, axis):
@@ -57,14 +57,14 @@
     return attn_heads.reshape(seq_rows, head_count * w_uv.shape[2]).astype(jnp.bfloat16)
 
 
-def to_same_core(rows, count):
+def to_group(rows, count):
     return lax.all_to_all(
         rows.reshape(count, -1, rows.shape[1]),
         "ep",
         split_axis=0,
         concat_axis=0,
         tiled=True,
-        axis_index_groups=same_core("ep"),
+        axis_index_groups=one_core_each("ep"),
     ).reshape(rows.shape)
 
 
@@ -134,7 +134,7 @@
         weights = jnp.where(placed(slots, at), expert_weight[:, None, :], 0.0).astype(jnp.bfloat16)
         return weights.reshape(expert_count * chunk, tok_rows).T
 
-    rows_a = to_same_core(sent_rows(slot, 0), expert_count)
+    rows_a = to_group(sent_rows(slot, 0), expert_count)
     slot_b, slot_back = lax.optimization_barrier((slot, slot))
     send_b = sent_rows(slot_b, 1)
     in_w = jnp.concatenate(
@@ -156,7 +156,7 @@
     part_a = activation_sums(rows_a, norm_gain, in_w)
     part_a, send_b = lax.optimization_barrier((part_a, send_b))
     share_a = row_shares(part_a)
-    rows_b = to_same_core(send_b, expert_count)
+    rows_b = to_group(send_b, expert_count)
     share_b = row_shares(activation_sums(rows_b, norm_gain, in_w))
     share_b, own_keys = lax.optimization_barrier((share_b, own_keys))
     all_keys = lax.all_gather(own_keys, "ctx", axis=1, tiled=True)
@@ -164,10 +164,10 @@
     attn_out = attention(q_latent, q_rope, lat_piece, rope_piece, w_uv)
     hidden_a = activations(share_a, model_width)
     out_a = jnp.dot(hidden_a, down_w, preferred_element_type=jnp.float32).astype(jnp.bfloat16)
-    back_a = to_same_core(out_a, expert_count)
+    back_a = to_group(out_a, expert_count)
     hidden_b = activations(share_b, model_width)
     out_b = jnp.dot(hidden_b, down_w, preferred_element_type=jnp.float32).astype(jnp.bfloat16)
-    back_b = to_same_core(out_b, expert_count)
+    back_b = to_group(out_b, expert_count)
     mixed = jnp.dot(weights_a, back_a, preferred_element_type=jnp.float32)
     moe_out = mixed + jnp.dot(weights_b, back_b, preferred_element_type=jnp.float32)
     moe_out = moe_out.astype(jnp.bfloat16)

time: 316 us -> 328 us (1.038)
  the two profiles are of different devices: /device:TPU:68 before, /device:TPU:65 now
where the time goes in v7:
time: 328 us; the launch traced here: 327 us
  waiting for transfers between devices  92.5 us (28%)
  blocking collectives  87.7 us (27%)
  starting transfers between devices  87.6 us (27%)
  matrix products  22.3 us (7%)
  between operations  14.1 us (4%)
  local copies, waits for them, and re-layouts  13.2 us (4%)
  other arithmetic  9.38 us (3%)
    all_to_all x3, starting transfers between devices, to_group(): lax.all_to_all(rows.reshape(count, -1, rows.shape[1]), 'ep', split_axis=0...  80.3 us
    all_to_all x3, waiting for transfers between devices, to_group(): lax.all_to_all(rows.reshape(count, -1, rows.shape[1]), 'ep', split_axis=0...  52.7 us
    all_to_all x1, blocking collectives, to_group(): lax.all_to_all(rows.reshape(count, -1, rows.shape[1]), 'ep', split_axis=0...  45 us
    all_gather x2, blocking collectives, activations(): return lax.all_gather(part_hidden, 'ctx', axis=0, tiled=True)  42.7 us
    reduce_scatter x2, waiting for transfers between devices, row_shares(): return lax.psum_scatter(in_part, 'ctx', scatter_dimension=0, tiled=True)  38.3 us
    unnamed x29, local copies, waits for them, and re-layouts  11.2 us
    dot_general x2, matrix products, activation_sums(): in_part = jnp.dot(gained, in_w, preferred_element_type=jnp.float32)  10.7 us
    ppermute x3, starting transfers between devices, of_other_core(): return lax.ppermute(value, axis, [(i, i ^ 1) for i in range(count)])  7.09 us
  transfers between devices with their start and end apart: 9, of which 5 were waited for; matrix products, arithmetic and copies ran while one was open for 9% of the time, Pallas kernels for 0%

profile of v7, /device:TPU:65, one launch (start us, length us, event | category | flops | bytes accessed | tf_op | source)
XLA Modules:
  0.0 326.8 jit_solution(10885797775252202024)
XLA Ops:
  8.4 2.3 convolution_convert_fusion.3
  10.7 44.8 %all-to-all-start = ((bf16[16,24,896]{2,1,0:T(8,128)(2,1)}), bf16[16,24,896]{2,1,0:T(8,128)(2,1)S(1)}, u32[]{:S(2)}, u32[]{:S(2)}) async-start(bf16[16,24,896]{2,1,0:T(8,128)(2,1)} %bitcast.4), calls=%async_computation | async-start | bytes 1376256 | tf_op jit(solution)/shard_map/all_to_all | solution.py:61
  55.6 2.7 collective-permute-start
  58.3 2.0 collective-permute-start.1
  60.3 2.4 collective-permute-start.2
  62.8 2.2 constant_dynamic-update-slice_fusion.3
  67.1 2.2 constant_dynamic-update-slice_fusion.2
  69.3 2.2 constant_dynamic-update-slice_fusion.1
  71.6 2.3 constant_dynamic-update-slice_fusion
  74.6 2.6 pad_maximum_fusion
  77.2 14.9 %all-to-all-done = bf16[16,24,896]{2,1,0:T(8,128)(2,1)S(1)} async-done(((bf16[16,24,896]{2,1,0:T(8,128)(2,1)}), bf16[16,24,896]{2,1,0:T(8,128)(2,1)S(1)}, u32[]{:S(2)}, u32[]{:S(2)}) %all-to-all-start) | async-done | bytes 688160 | tf_op jit(solution)/shard_map/all_to_all | solution.py:61
  92.3 5.3 %fusion = bf16[384,2176]{1,0:T(8,128)(2,1)} fusion(bf16[896,2176]{1,0:T(8,128)(2,1)} %broadcast_dynamic-update-slice_fusion, bf16[384]{0:T(512)(128)(2,1)S(1)} %fusion.5, pred[2176]{0:T(1024)(128)(4,1)S(1)} %iota_compare_fusion.5, bf16[384,896]{1,0:T(8,128)(2,1)S(1)} %bitcast.83, f32[896]{0:T(1024)S(1)} %copy-done.9), kind=kOutput, calls=%fused_computation.2 | convolution fusion | flops 1499234304 | bytes 6265216 | tf_op jit(solution)/shard_map/dot_general | solution.py:75
  97.6 45.0 %all_to_all.20 = bf16[16,24,896]{2,1,0:T(8,128)(2,1)S(1)} all-to-all(bf16[16,24,896]{2,1,0:T(8,128)(2,1)S(1)} %bitcast.85), channel_id=1, replica_groups={{0,3,4,7,8,11,12,15,16,19,20,23,24,27,28,31},{1,2,5,6,9,10,13,14,17,18,..., dimensions={0} | all-to-all | bytes 1376256 | tf_op jit(solution)/shard_map/all_to_all | solution.py:61
  143.0 5.4 %fusion.1 = bf16[384,2176]{1,0:T(8,128)(2,1)} fusion(bf16[384,896]{1,0:T(8,128)(2,1)S(1)} %fusion.6, bf16[896,2176]{1,0:T(8,128)(2,1)} %broadcast_dynamic-update-slice_fusion, bf16[384]{0:T(512)(128)(2,1)S(1)} %broadcast_in_dim.107, pred[2176]{0:T(1024)(128)(4,1)S(1)} %iota_compare_fusion.5), kind=kOutput, calls=%fused_computation.3 | convolution fusion | flops 1498202112 | bytes 6261632 | tf_op jit(solution)/shard_map/dot_general | solution.py:75
  149.3 36.6 %reduce-scatter.3.cloned.1.call-done = bf16[48,2176]{1,0:T(8,128)(2,1)} async-done(((bf16[384,2176]{1,0:T(8,128)(2,1)}), bf16[48,2176]{1,0:T(8,128)(2,1)}) %reduce-scatter.3.cloned.1.call-update) | async-done | bytes 208912 | tf_op jit(solution)/shard_map/reduce_scatter | solution.py:81
  187.8 20.8 %all_gather.11 = bf16[384,1024]{1,0:T(8,128)(2,1)S(1)} all-gather(bf16[48,1024]{1,0:T(8,128)(2,1)S(1)} %multiply_convert_fusion), channel_id=1, replica_groups=mesh['group'=2,'ctx'=8,'ep'=32] {'ctx'}, dimensions={0}, use_global_device_ids=true | all-gather | bytes 884736 | tf_op jit(solution)/shard_map/all_gather | solution.py:90
  208.6 1.9 convolution_convert_fusion
  210.5 22.5 %all-to-all-start.3 = ((bf16[16,24,896]{2,1,0:T(8,128)(2,1)}), bf16[16,24,896]{2,1,0:T(8,128)(2,1)S(1)}, u32[]{:S(2)}, u32[]{:S(2)}) async-start(bf16[16,24,896]{2,1,0:T(8,128)(2,1)} %bitcast.92), calls=%async_computation.5 | async-start | bytes 1376256 | tf_op jit(solution)/shard_map/all_to_all | solution.py:61
  233.8 1.8 reduce-scatter.5.cloned.1.call-done
  237.6 21.9 %all_gather.10 = bf16[384,1024]{1,0:T(8,128)(2,1)S(1)} all-gather(bf16[48,1024]{1,0:T(8,128)(2,1)S(1)} %multiply_convert_fusion.1), channel_id=1, replica_groups=mesh['group'=2,'ctx'=8,'ep'=32] {'ctx'}, dimensions={0}, use_global_device_ids=true | all-gather | bytes 884736 | tf_op jit(solution)/shard_map/all_gather | solution.py:90
  259.5 1.8 convolution_convert_fusion.1
  261.3 8.2 %all-to-all-done.3 = bf16[16,24,896]{2,1,0:T(8,128)(2,1)S(1)} async-done(((bf16[16,24,896]{2,1,0:T(8,128)(2,1)}), bf16[16,24,896]{2,1,0:T(8,128)(2,1)S(1)}, u32[]{:S(2)}, u32[]{:S(2)}) %all-to-all-start.3) | async-done | bytes 688160 | tf_op jit(solution)/shard_map/all_to_all | solution.py:61
  269.5 13.0 %all-to-all-start.2 = ((bf16[16,24,896]{2,1,0:T(8,128)(2,1)}), bf16[16,24,896]{2,1,0:T(8,128)(2,1)S(1)}, u32[]{:S(2)}, u32[]{:S(2)}) async-start(bf16[16,24,896]{2,1,0:T(8,128)(2,1)} %bitcast.91), calls=%async_computation.4 | async-start | bytes 1376256 | tf_op jit(solution)/shard_map/all_to_all | solution.py:61
  289.5 29.5 %all-to-all-done.2 = bf16[16,24,896]{2,1,0:T(8,128)(2,1)S(1)} async-done(((bf16[16,24,896]{2,1,0:T(8,128)(2,1)}), bf16[16,24,896]{2,1,0:T(8,128)(2,1)S(1)}, u32[]{:S(2)}, u32[]{:S(2)}) %all-to-all-start.2) | async-done | bytes 688160 | tf_op jit(solution)/shard_map/all_to_all | solution.py:61
  (69 shorter events, 18.5 us)
Async XLA Ops:
  7.2 280.8 %copy-start = (bf16[4,512,128]{2,1,0:T(8,128)(2,1)S(1)}, bf16[4,512,128]{2,1,0:T(8,128)(2,1)}, u32[]{:S(2)}) copy-start(bf16[4,512,128]{2,1,0:T(8,128)(2,1)} %param.16) | copy-start | bytes 1572868
  7.2 53.1 %copy-start.3 = (bf16[1,512,896]{2,1,0:T(8,128)(2,1)S(1)}, bf16[1,512,896]{2,1,0:T(8,128)(2,1)}, u32[]{:S(2)}) copy-start(bf16[1,512,896]{2,1,0:T(8,128)(2,1)} %param.23) | copy-start | bytes 2752516
  7.2 55.5 %copy-start.10 = (f32[256,2]{0,1:T(2,128)S(1)}, f32[256,2]{0,1:T(2,128)}, u32[]{:S(2)}) copy-start(f32[256,2]{0,1:T(2,128)} %param.20) | copy-start | bytes 6148
  8.4 56.6 %copy-start.5 = (bf16[512,128]{1,0:T(8,128)(2,1)S(1)}, bf16[512,128]{1,0:T(8,128)(2,1)}, u32[]{:S(2)}) copy-start(bf16[512,128]{1,0:T(8,128)(2,1)} %param.14) | copy-start | bytes 393220
  8.4 56.6 %copy-start.7 = (bf16[64,128]{1,0:T(8,128)(2,1)S(1)}, bf16[64,128]{1,0:T(8,128)(2,1)}, u32[]{:S(2)}) copy-start(bf16[64,128]{1,0:T(8,128)(2,1)} %param.15) | copy-start | bytes 49156
  10.7 56.1 %copy-start.2 = (bf16[256,896]{1,0:T(8,128)(2,1)S(1)}, bf16[256,896]{1,0:T(8,128)(2,1)}, u32[]{:S(2)}) copy-start(bf16[256,896]{1,0:T(8,128)(2,1)} %param.17) | copy-start | bytes 1376260
  10.7 81.4 %all-to-all-start = ((bf16[16,24,896]{2,1,0:T(8,128)(2,1)}), bf16[16,24,896]{2,1,0:T(8,128)(2,1)S(1)}, u32[]{:S(2)}, u32[]{:S(2)}) async-start(bf16[16,24,896]{2,1,0:T(8,128)(2,1)} %bitcast.4), calls=%async_computation | async-start | bytes 1376256 | tf_op jit(solution)/shard_map/all_to_all | solution.py:61
  55.6 130.3 %reduce-scatter.3.cloned.1.call-start = ((), (), s32[]{:S(2)}) async-start(), calls=%async_computation.6 | async-start | bytes 1880064 | tf_op jit(solution)/shard_map/reduce_scatter | solution.py:81
  55.6 11.5 %collective-permute-start = (bf16[896,512]{1,0:T(8,128)(2,1)}, bf16[896,512]{1,0:T(8,128)(2,1)}, u32[]{:S(2)}, u32[]{:S(2)}) collective-permute-start(bf16[896,512]{1,0:T(8,128)(2,1)} %bitcast.7), channel_id=1, source_target_pairs={{0,1},{1,0},{2,3},{3,2},{4,5},{5,4},{6,7},{7,6},{8,9},{9,8},{10,11... | collective-permute-start | bytes 2752520 | tf_op jit(solution)/shard_map/ppermute | solution.py:19
  58.3 13.2 %collective-permute-start.1 = (bf16[896,512]{1,0:T(8,128)(2,1)}, bf16[896,512]{1,0:T(8,128)(2,1)}, u32[]{:S(2)}, u32[]{:S(2)}) collective-permute-start(bf16[896,512]{1,0:T(8,128)(2,1)} %bitcast.8), channel_id=1, source_target_pairs={{0,1},{1,0},{2,3},{3,2},{4,5},{5,4},{6,7},{7,6},{8,9},{9,8},{10,11... | collective-permute-start | bytes 2752520 | tf_op jit(solution)/shard_map/ppermute | solution.py:19
  60.3 14.3 %collective-permute-start.2 = (bf16[512,896]{1,0:T(8,128)(2,1)S(1)}, bf16[512,896]{1,0:T(8,128)(2,1)}, u32[]{:S(2)}, u32[]{:S(2)}) collective-permute-start(bf16[512,896]{1,0:T(8,128)(2,1)S(1)} %bitcast.87), channel_id=1, source_target_pairs={{0,1},{1,0},{2,3},{3,2},{4,5},{5,4},{6,7},{7,6},{8,9},{9,8},{10,11... | collective-permute-start | bytes 2752520 | tf_op jit(solution)/shard_map/ppermute | solution.py:19
  74.6 17.8 %copy-start.9 = (f32[896]{0:T(1024)S(1)}, f32[896]{0:T(1024)}, u32[]{:S(2)}) copy-start(f32[896]{0:T(1024)} %param.18) | copy-start | bytes 10756
  148.4 60.2 %copy-start.1 = (bf16[1024,896]{1,0:T(8,128)(2,1)S(1)}, bf16[1024,896]{1,0:T(8,128)(2,1)}, u32[]{:S(2)}) copy-start(bf16[1024,896]{1,0:T(8,128)(2,1)} %pad_maximum_fusion) | copy-start | bytes 5505028
  148.5 87.1 %reduce-scatter.5.cloned.1.call-start = ((), (), s32[]{:S(2)}) async-start(), calls=%async_computation.8 | async-start | bytes 1880064 | tf_op jit(solution)/shard_map/reduce_scatter | solution.py:81
  210.5 59.0 %all-to-all-start.3 = ((bf16[16,24,896]{2,1,0:T(8,128)(2,1)}), bf16[16,24,896]{2,1,0:T(8,128)(2,1)S(1)}, u32[]{:S(2)}, u32[]{:S(2)}) async-start(bf16[16,24,896]{2,1,0:T(8,128)(2,1)} %bitcast.92), calls=%async_computation.5 | async-start | bytes 1376256 | tf_op jit(solution)/shard_map/all_to_all | solution.py:61
  233.0 51.2 %all-gather.2.cloned.1.call-start = ((), (), s32[]{:S(2)}) async-start(), calls=%async_computation.7 | async-start | bytes 1327104 | tf_op jit(solution)/shard_map/all_gather | solution.py:162
  259.5 23.0 %copy-start.6 = (bf16[128,256]{1,0:T(8,128)(2,1)S(1)}, bf16[128,256]{1,0:T(8,128)(2,1)}, u32[]{:S(2)}) copy-start(bf16[128,256]{1,0:T(8,128)(2,1)} %param.13) | copy-start | bytes 196612
  269.5 49.5 %all-to-all-start.2 = ((bf16[16,24,896]{2,1,0:T(8,128)(2,1)}), bf16[16,24,896]{2,1,0:T(8,128)(2,1)S(1)}, u32[]{:S(2)}, u32[]{:S(2)}) async-start(bf16[16,24,896]{2,1,0:T(8,128)(2,1)} %bitcast.91), calls=%async_computation.4 | async-start | bytes 1376256 | tf_op jit(solution)/shard_map/all_to_all | solution.py:61
  284.2 1.5 copy-start.8
  287.2 1.9 copy-start.4
Sparse Core Ops, SparseCore 0:
  148.6 37.2 reduce-scatter.2
  188.7 46.8 reduce-scatter.4
  237.6 45.9 all-gather.1
